TPU v7x, 16 devices: a 4x2x1 block of a 4x4x8 slice. The times are simulated.
16 devices in a mesh: dp: 2 (over y, z), ctx: 8 (over x, core).
Axes of the slice: x: 4, y: 2, z: 1, core: 2. Of those that a mesh axis runs over, the one named last changes fastest.
The devices are a block of a 4x4x8 slice.
Arguments:
- q_seq: bfloat16 [2, 8192, 8, 256], P('dp', 'ctx'), parts along dimension 0
- k_seq: bfloat16 [2, 8192, 4, 256], P('dp', 'ctx'), parts along dimension 0
- v_seq: bfloat16 [2, 8192, 4, 256], P('dp', 'ctx'), parts along dimension 0
- do_seq: bfloat16 [2, 8192, 8, 256], P('dp', 'ctx'), parts along dimension 0
Outputs:
- output 1: bfloat16 [2, 8192, 8, 256], P('dp', 'ctx'), parts along dimension 0
- output 2: bfloat16 [2, 8192, 8, 256], P('dp', 'ctx'), parts along dimension 0
- output 3: bfloat16 [2, 8192, 4, 256], P('dp', 'ctx'), parts along dimension 0
- output 4: bfloat16 [2, 8192, 4, 256], P('dp', 'ctx'), parts along dimension 0
There are 2 independent parts. A program takes and returns all parts, laid end to end along the dimension named above; each array names one.
All inputs are finite; a program needn't handle non-finite values.
Results may differ from a plain program's by a relative error of at most 0.00872058.
Values are sent between devices in bfloat16 or wider.
A program may use at most 768 MiB of HBM per device.

v0:
```python
import jax
import jax.numpy as jnp
from jax import lax
from jax.sharding import PartitionSpec as P

WINDOW = 4096
NEG_BIG = -1e30


def fwd_update(state, q_five, k_blk, v_blk, keep_mask, sm_scale):
    m_run, l_run, o_acc = state
    scores = jnp.einsum('bqhgd,bkhd->bhgqk', q_five, k_blk, preferred_element_type=jnp.float32) * sm_scale
    scores = jnp.where(keep_mask, scores, NEG_BIG)
    m_new = jnp.maximum(m_run, jnp.max(scores, axis=-1))
    rescale = jnp.exp(m_run - m_new)
    p_blk = jnp.exp(scores - m_new[..., None])
    l_new = rescale * l_run + jnp.sum(p_blk, axis=-1)
    pv_blk = jnp.einsum('bhgqk,bkhd->bhgqd', p_blk.astype(jnp.bfloat16), v_blk, preferred_element_type=jnp.float32)
    return m_new, l_new, rescale[..., None] * o_acc + pv_blk


def bwd_block(q_five, do_five, log_sum, d_row, k_blk, v_blk, keep_mask, sm_scale):
    scores = jnp.einsum('bqhgd,bkhd->bhgqk', q_five, k_blk, preferred_element_type=jnp.float32) * sm_scale
    p_blk = jnp.exp(jnp.where(keep_mask, scores, NEG_BIG) - log_sum[..., None])
    d_prob = jnp.einsum('bqhgd,bkhd->bhgqk', do_five, v_blk, preferred_element_type=jnp.float32)
    d_score = (p_blk * (d_prob - d_row[..., None])).astype(jnp.bfloat16)
    dv_part = jnp.einsum('bhgqk,bqhgd->bkhd', p_blk.astype(jnp.bfloat16), do_five, preferred_element_type=jnp.float32)
    dq_part = jnp.einsum('bhgqk,bkhd->bqhgd', d_score, k_blk, preferred_element_type=jnp.float32) * sm_scale
    dk_part = jnp.einsum('bhgqk,bqhgd->bkhd', d_score, q_five, preferred_element_type=jnp.float32) * sm_scale
    return dq_part, dk_part, dv_part


def solution(mesh):
    n_ctx = mesh.shape['ctx']
    seq_spec = P('dp', 'ctx', None, None)
    shift_perm = [(j, (j + 1) % n_ctx) for j in range(n_ctx)]

    def local_attn(q_loc, k_loc, v_loc, do_loc):
        n_batch, chunk_len, q_heads, head_dim = q_loc.shape
        kv_heads = k_loc.shape[2]
        q_group = q_heads // kv_heads
        n_blocks = WINDOW // chunk_len
        sm_scale = head_dim ** -0.5
        dev_idx = lax.axis_index('ctx')
        five_shape = (n_batch, chunk_len, kv_heads, q_group, head_dim)
        q_five = q_loc.reshape(five_shape)
        do_five = do_loc.reshape(five_shape)
        offsets = jnp.arange(chunk_len)[:, None] - jnp.arange(chunk_len)[None, :]

        def block_mask(step_id):
            dist = step_id * chunk_len + offsets
            return (dist >= 0) & (dist < WINDOW) & (dev_idx >= step_id)

        stat_shape = (n_batch, kv_heads, q_group, chunk_len)
        init = (jnp.full(stat_shape, NEG_BIG, jnp.float32), jnp.zeros(stat_shape, jnp.float32), jnp.zeros(stat_shape + (head_dim,), jnp.float32))
        state = fwd_update(init, q_five, k_loc, v_loc, block_mask(0), sm_scale)

        def fwd_body(step_id, carry):
            kv_blk, run_state = carry
            kv_blk = lax.ppermute(kv_blk, 'ctx', shift_perm)
            run_state = fwd_update(run_state, q_five, kv_blk[0], kv_blk[1], block_mask(step_id), sm_scale)
            return kv_blk, run_state

        _, (m_run, l_run, o_acc) = lax.fori_loop(1, n_blocks + 1, fwd_body, ((k_loc, v_loc), state))
        log_sum = m_run + jnp.log(l_run)
        o_five = jnp.transpose((o_acc / l_run[..., None]).astype(jnp.bfloat16), (0, 3, 1, 2, 4))
        d_row = jnp.einsum('bqhgd,bqhgd->bhgq', do_five, o_five, preferred_element_type=jnp.float32)
        dq_acc, dk_acc, dv_acc = bwd_block(q_five, do_five, log_sum, d_row, k_loc, v_loc, block_mask(0), sm_scale)

        def bwd_body(step_id, carry):
            travel, dq_run = carry
            k_blk, v_blk, dk_run, dv_run = lax.ppermute(travel, 'ctx', shift_perm)
            dq_part, dk_part, dv_part = bwd_block(q_five, do_five, log_sum, d_row, k_blk, v_blk, block_mask(step_id), sm_scale)
            return (k_blk, v_blk, dk_run + dk_part, dv_run + dv_part), dq_run + dq_part

        (_, _, dk_acc, dv_acc), dq_acc = lax.fori_loop(1, n_blocks + 1, bwd_body, ((k_loc, v_loc, dk_acc, dv_acc), dq_acc))
        home_perm = [(j, (j - n_blocks) % n_ctx) for j in range(n_ctx)]
        dk_home, dv_home = lax.ppermute((dk_acc, dv_acc), 'ctx', home_perm)
        return (o_five.reshape(q_loc.shape), dq_acc.astype(jnp.bfloat16).reshape(q_loc.shape), dk_home.astype(jnp.bfloat16), dv_home.astype(jnp.bfloat16))

    return jax.shard_map(local_attn, mesh=mesh, in_specs=(seq_spec, seq_spec, seq_spec, seq_spec), out_specs=(seq_spec, seq_spec, seq_spec, seq_spec), check_vma=False)
```

profile of v0, /device:TPU:113, one launch (start us, length us, event | category | flops | bytes accessed | tf_op | source)
XLA Modules:
  0.0 1195.2 jit_solution(8989038227379152420)
XLA Ops:
  67.4 319.5 %while.44 = (s32[]{:T(128)}, bf16[1,1024,4,256]{3,1,2,0:T(8,128)(2,1)}, bf16[1,1024,4,256]{3,1,2,0:T(8,128)(2,1)}, f32[1,4,2,1024]{3,2,1,0:T(2,128)S(1)}, f32[1,...) while((s32[]{:T(128)}, ...), condition=%wide.region_5.6_spmd.clone, body=%wide.region_2.5_spmd.clone.sunk | while | flops 8692719616 | bytes 214434080 | solution.py:64
  72.0 21.5 %collective-permute-done = bf16[1,1024,4,256]{3,1,2,0:T(8,128)(2,1)} collective-permute-done((bf16[1,1024,4,256]{3,1,2,0:T(8,128)(2,1)}, bf16[1,1024,4,256]{3,1,2,0:T(8,128)(2,1)}, u32[]{:S(2)}, u32[]{:S(2)}) %collective-permute-start) | collective-permute-done | bytes 2097184 | tf_op jit(solution)/shard_map/while/body/eval_jaxpr/ppermute | solution.py:60
  151.7 21.5 %collective-permute-done = bf16[1,1024,4,256]{3,1,2,0:T(8,128)(2,1)} collective-permute-done((bf16[1,1024,4,256]{3,1,2,0:T(8,128)(2,1)}, bf16[1,1024,4,256]{3,1,2,0:T(8,128)(2,1)}, u32[]{:S(2)}, u32[]{:S(2)}) %collective-permute-start) | collective-permute-done | bytes 2097184 | tf_op jit(solution)/shard_map/while/body/eval_jaxpr/ppermute | solution.py:60
  231.4 21.5 %collective-permute-done = bf16[1,1024,4,256]{3,1,2,0:T(8,128)(2,1)} collective-permute-done((bf16[1,1024,4,256]{3,1,2,0:T(8,128)(2,1)}, bf16[1,1024,4,256]{3,1,2,0:T(8,128)(2,1)}, u32[]{:S(2)}, u32[]{:S(2)}) %collective-permute-start) | collective-permute-done | bytes 2097184 | tf_op jit(solution)/shard_map/while/body/eval_jaxpr/ppermute | solution.py:60
  311.1 21.5 %collective-permute-done = bf16[1,1024,4,256]{3,1,2,0:T(8,128)(2,1)} collective-permute-done((bf16[1,1024,4,256]{3,1,2,0:T(8,128)(2,1)}, bf16[1,1024,4,256]{3,1,2,0:T(8,128)(2,1)}, u32[]{:S(2)}, u32[]{:S(2)}) %collective-permute-start) | collective-permute-done | bytes 2097184 | tf_op jit(solution)/shard_map/while/body/eval_jaxpr/ppermute | solution.py:60
  419.6 25.4 %fusion.68 = bf16[4,2,1024,1024]{2,3,1,0:T(8,128)(2,1)} fusion(f32[4,1024,1024,2]{2,1,3,0:T(8,128)} %get-tuple-element.476, f32[4,2,1024]{2,1,0:T(2,128)S(1)} %copy.48, f32[4,2,1024]{2,1,0:T(2,128)S(1)} %bitcast.340, pred[1024,1024]{0,1:T(8,128)(4,1)S(1)} %copy-done.10, bf16[1024,4,2,256]{3,2,1,0:T(2,128)(2,1)} %reshape.253, ...), kind=kOutput, calls=%fused_computation.73 | convolution fusion | flops 4345298944 | bytes 57737216 | tf_op jit(solution)/shard_map/bqhgd,bkhd->bhgqk/dot_general | solution.py:25
  471.2 626.3 %while.45 = (s32[]{:T(128)}, bf16[1,1024,4,256]{3,1,2,0:T(8,128)(2,1)}, bf16[1,1024,4,256]{3,1,2,0:T(8,128)(2,1)}, f32[1,1024,4,256]{3,1,2,0:T(8,128)}, f32[1,10...) while((s32[]{:T(128)}, ...), condition=%wide.region_7.8_spmd.clone, body=%wide.region_6.7_spmd.clone.sunk | while | flops 21572354048 | bytes 269582624 | solution.py:76
  477.1 19.7 %collective-permute-done.2 = bf16[1,1024,4,256]{3,1,2,0:T(8,128)(2,1)S(1)} collective-permute-done((bf16[1,1024,4,256]{3,1,2,0:T(8,128)(2,1)}, bf16[1,1024,4,256]{3,1,2,0:T(8,128)(2,1)S(1)}, u32[]{:S(2)}, u32[]{:S(2)}) %collective-permute-start.2) | collective-permute-done | bytes 2097184 | tf_op jit(solution)/shard_map/while/body/eval_jaxpr/ppermute | solution.py:72
  519.3 23.8 %fusion.143 = bf16[4,2,1024,1024]{2,3,1,0:T(8,128)(2,1)} fusion(f32[4,1024,1024,2]{2,1,3,0:T(8,128)} %fusion.141, f32[4,2,1024]{2,1,0:T(2,128)S(1)} %bitcast.338, f32[4,2,1024]{2,1,0:T(2,128)S(1)} %bitcast.342, pred[1024,1024]{0,1:T(8,128)(4,1)S(1)} %fusion.142, bf16[1,1024,4,2,256]{4,1,3,2,0:T(8,128)(2,1)} %get-tuple-element.666, ...), kind=kOutput, calls=%fused_computation.37.clone.1 | convolution fusion | flops 4345298944 | bytes 57737216 | tf_op jit(solution)/shard_map/while/body/eval_jaxpr/bqhgd,bkhd->bhgqk/dot_general | solution.py:25
  578.9 30.2 %collective-permute-done.5 = f32[1,1024,4,256]{3,1,2,0:T(8,128)} collective-permute-done((f32[1,1024,4,256]{3,1,2,0:T(8,128)}, f32[1,1024,4,256]{3,1,2,0:T(8,128)}, u32[]{:S(2)}, u32[]{:S(2)}) %collective-permute-start.5) | collective-permute-done | bytes 4194336 | tf_op jit(solution)/shard_map/while/body/eval_jaxpr/ppermute | solution.py:72
  609.2 18.7 %bitcast_add_fusion.14 = f32[1,1024,4,256]{3,1,2,0:T(8,128)} fusion(f32[1,1024,4,256]{3,1,2,0:T(8,128)} %collective-permute-done.5, bf16[1,1024,4,2,256]{4,1,3,2,0:T(8,128)(2,1)} %get-tuple-element.666, f32[4,1024,1024,2]{2,1,3,0:T(8,128)} %fusion.141, f32[4,2,1024]{2,1,0:T(2,128)S(1)} %bitcast.343, pred[1024,1024]{0,1:T(8,128)(4,1)S(1)} %fusion.142), kind=kOutput, calls=%fused_computation.41.clone.1 | convolution fusion | flops 4329570304 | bytes 47218688 | tf_op jit(solution)/shard_map/while/body/eval_jaxpr/bhgqk,bqhgd->bkhd/dot_general | solution.py:27
  633.5 19.8 %collective-permute-done.2 = bf16[1,1024,4,256]{3,1,2,0:T(8,128)(2,1)S(1)} collective-permute-done((bf16[1,1024,4,256]{3,1,2,0:T(8,128)(2,1)}, bf16[1,1024,4,256]{3,1,2,0:T(8,128)(2,1)S(1)}, u32[]{:S(2)}, u32[]{:S(2)}) %collective-permute-start.2) | collective-permute-done | bytes 2097184 | tf_op jit(solution)/shard_map/while/body/eval_jaxpr/ppermute | solution.py:72
  675.8 23.8 %fusion.143 = bf16[4,2,1024,1024]{2,3,1,0:T(8,128)(2,1)} fusion(f32[4,1024,1024,2]{2,1,3,0:T(8,128)} %fusion.141, f32[4,2,1024]{2,1,0:T(2,128)S(1)} %bitcast.338, f32[4,2,1024]{2,1,0:T(2,128)S(1)} %bitcast.342, pred[1024,1024]{0,1:T(8,128)(4,1)S(1)} %fusion.142, bf16[1,1024,4,2,256]{4,1,3,2,0:T(8,128)(2,1)} %get-tuple-element.666, ...), kind=kOutput, calls=%fused_computation.37.clone.1 | convolution fusion | flops 4345298944 | bytes 57737216 | tf_op jit(solution)/shard_map/while/body/eval_jaxpr/bqhgd,bkhd->bhgqk/dot_general | solution.py:25
  735.4 30.2 %collective-permute-done.5 = f32[1,1024,4,256]{3,1,2,0:T(8,128)} collective-permute-done((f32[1,1024,4,256]{3,1,2,0:T(8,128)}, f32[1,1024,4,256]{3,1,2,0:T(8,128)}, u32[]{:S(2)}, u32[]{:S(2)}) %collective-permute-start.5) | collective-permute-done | bytes 4194336 | tf_op jit(solution)/shard_map/while/body/eval_jaxpr/ppermute | solution.py:72
  765.7 18.7 %bitcast_add_fusion.14 = f32[1,1024,4,256]{3,1,2,0:T(8,128)} fusion(f32[1,1024,4,256]{3,1,2,0:T(8,128)} %collective-permute-done.5, bf16[1,1024,4,2,256]{4,1,3,2,0:T(8,128)(2,1)} %get-tuple-element.666, f32[4,1024,1024,2]{2,1,3,0:T(8,128)} %fusion.141, f32[4,2,1024]{2,1,0:T(2,128)S(1)} %bitcast.343, pred[1024,1024]{0,1:T(8,128)(4,1)S(1)} %fusion.142), kind=kOutput, calls=%fused_computation.41.clone.1 | convolution fusion | flops 4329570304 | bytes 47218688 | tf_op jit(solution)/shard_map/while/body/eval_jaxpr/bhgqk,bqhgd->bkhd/dot_general | solution.py:27
  790.0 19.8 %collective-permute-done.2 = bf16[1,1024,4,256]{3,1,2,0:T(8,128)(2,1)S(1)} collective-permute-done((bf16[1,1024,4,256]{3,1,2,0:T(8,128)(2,1)}, bf16[1,1024,4,256]{3,1,2,0:T(8,128)(2,1)S(1)}, u32[]{:S(2)}, u32[]{:S(2)}) %collective-permute-start.2) | collective-permute-done | bytes 2097184 | tf_op jit(solution)/shard_map/while/body/eval_jaxpr/ppermute | solution.py:72
  832.3 23.8 %fusion.143 = bf16[4,2,1024,1024]{2,3,1,0:T(8,128)(2,1)} fusion(f32[4,1024,1024,2]{2,1,3,0:T(8,128)} %fusion.141, f32[4,2,1024]{2,1,0:T(2,128)S(1)} %bitcast.338, f32[4,2,1024]{2,1,0:T(2,128)S(1)} %bitcast.342, pred[1024,1024]{0,1:T(8,128)(4,1)S(1)} %fusion.142, bf16[1,1024,4,2,256]{4,1,3,2,0:T(8,128)(2,1)} %get-tuple-element.666, ...), kind=kOutput, calls=%fused_computation.37.clone.1 | convolution fusion | flops 4345298944 | bytes 57737216 | tf_op jit(solution)/shard_map/while/body/eval_jaxpr/bqhgd,bkhd->bhgqk/dot_general | solution.py:25
  891.9 30.2 %collective-permute-done.5 = f32[1,1024,4,256]{3,1,2,0:T(8,128)} collective-permute-done((f32[1,1024,4,256]{3,1,2,0:T(8,128)}, f32[1,1024,4,256]{3,1,2,0:T(8,128)}, u32[]{:S(2)}, u32[]{:S(2)}) %collective-permute-start.5) | collective-permute-done | bytes 4194336 | tf_op jit(solution)/shard_map/while/body/eval_jaxpr/ppermute | solution.py:72
  946.5 19.8 %collective-permute-done.2 = bf16[1,1024,4,256]{3,1,2,0:T(8,128)(2,1)S(1)} collective-permute-done((bf16[1,1024,4,256]{3,1,2,0:T(8,128)(2,1)}, bf16[1,1024,4,256]{3,1,2,0:T(8,128)(2,1)S(1)}, u32[]{:S(2)}, u32[]{:S(2)}) %collective-permute-start.2) | collective-permute-done | bytes 2097184 | tf_op jit(solution)/shard_map/while/body/eval_jaxpr/ppermute | solution.py:72
  988.7 23.8 %fusion.143 = bf16[4,2,1024,1024]{2,3,1,0:T(8,128)(2,1)} fusion(f32[4,1024,1024,2]{2,1,3,0:T(8,128)} %fusion.141, f32[4,2,1024]{2,1,0:T(2,128)S(1)} %bitcast.338, f32[4,2,1024]{2,1,0:T(2,128)S(1)} %bitcast.342, pred[1024,1024]{0,1:T(8,128)(4,1)S(1)} %fusion.142, bf16[1,1024,4,2,256]{4,1,3,2,0:T(8,128)(2,1)} %get-tuple-element.666, ...), kind=kOutput, calls=%fused_computation.37.clone.1 | convolution fusion | flops 4345298944 | bytes 57737216 | tf_op jit(solution)/shard_map/while/body/eval_jaxpr/bqhgd,bkhd->bhgqk/dot_general | solution.py:25
  1048.4 30.2 %collective-permute-done.5 = f32[1,1024,4,256]{3,1,2,0:T(8,128)} collective-permute-done((f32[1,1024,4,256]{3,1,2,0:T(8,128)}, f32[1,1024,4,256]{3,1,2,0:T(8,128)}, u32[]{:S(2)}, u32[]{:S(2)}) %collective-permute-start.5) | collective-permute-done | bytes 4194336 | tf_op jit(solution)/shard_map/while/body/eval_jaxpr/ppermute | solution.py:72
  1078.6 18.7 %bitcast_add_fusion.14 = f32[1,1024,4,256]{3,1,2,0:T(8,128)} fusion(f32[1,1024,4,256]{3,1,2,0:T(8,128)} %collective-permute-done.5, bf16[1,1024,4,2,256]{4,1,3,2,0:T(8,128)(2,1)} %get-tuple-element.666, f32[4,1024,1024,2]{2,1,3,0:T(8,128)} %fusion.141, f32[4,2,1024]{2,1,0:T(2,128)S(1)} %bitcast.343, pred[1024,1024]{0,1:T(8,128)(4,1)S(1)} %fusion.142), kind=kOutput, calls=%fused_computation.41.clone.1 | convolution fusion | flops 4329570304 | bytes 47218688 | tf_op jit(solution)/shard_map/while/body/eval_jaxpr/bhgqk,bqhgd->bkhd/dot_general | solution.py:27
  1119.9 22.7 %collective-permute-done.6 = bf16[1,1024,4,256]{3,2,1,0:T(4,128)(2,1)} collective-permute-done((bf16[1,1024,4,256]{3,2,1,0:T(4,128)(2,1)S(1)}, bf16[1,1024,4,256]{3,2,1,0:T(4,128)(2,1)}, u32[]{:S(2)}, u32[]{:S(2)}) %collective-permute-start.6) | collective-permute-done | bytes 2097184 | tf_op jit(solution)/shard_map/ppermute | solution.py:78
  1142.6 44.9 %collective-permute-done.7 = bf16[1,1024,4,256]{3,2,1,0:T(4,128)(2,1)} collective-permute-done((bf16[1,1024,4,256]{3,2,1,0:T(4,128)(2,1)S(1)}, bf16[1,1024,4,256]{3,2,1,0:T(4,128)(2,1)}, u32[]{:S(2)}, u32[]{:S(2)}) %collective-permute-start.7) | collective-permute-done | bytes 2097184 | tf_op jit(solution)/shard_map/ppermute | solution.py:78
  (180 shorter events, 662.6 us)
Async XLA Ops:
  67.8 25.7 %collective-permute-start = (bf16[1,1024,4,256]{3,1,2,0:T(8,128)(2,1)}, bf16[1,1024,4,256]{3,1,2,0:T(8,128)(2,1)}, u32[]{:S(2)}, u32[]{:S(2)}) collective-permute-start(bf16[1,1024,4,256]{3,1,2,0:T(8,128)(2,1)} %get-tuple-element.612), channel_id=1, source_target_pairs={{0,1},{1,2},{2,3},{3,4},{4,5},{5,6},{6,7},{7,0},{8,9},{9,10},{10,1... | collective-permute-start | bytes 6291464 | tf_op jit(solution)/shard_map/while/body/eval_jaxpr/ppermute | solution.py:60
  70.5 57.7 %collective-permute-start.1 = (bf16[1,1024,4,256]{3,1,2,0:T(8,128)(2,1)}, bf16[1,1024,4,256]{3,1,2,0:T(8,128)(2,1)S(1)}, u32[]{:S(2)}, u32[]{:S(2)}) collective-permute-start(bf16[1,1024,4,256]{3,1,2,0:T(8,128)(2,1)} %get-tuple-element.613), channel_id=1, source_target_pairs={{0,1},{1,2},{2,3},{3,4},{4,5},{5,6},{6,7},{7,0},{8,9},{9,10},{10,1... | collective-permute-start | bytes 6291464 | tf_op jit(solution)/shard_map/while/body/eval_jaxpr/ppermute | solution.py:60
  150.2 57.7 %collective-permute-start.1 = (bf16[1,1024,4,256]{3,1,2,0:T(8,128)(2,1)}, bf16[1,1024,4,256]{3,1,2,0:T(8,128)(2,1)S(1)}, u32[]{:S(2)}, u32[]{:S(2)}) collective-permute-start(bf16[1,1024,4,256]{3,1,2,0:T(8,128)(2,1)} %get-tuple-element.613), channel_id=1, source_target_pairs={{0,1},{1,2},{2,3},{3,4},{4,5},{5,6},{6,7},{7,0},{8,9},{9,10},{10,1... | collective-permute-start | bytes 6291464 | tf_op jit(solution)/shard_map/while/body/eval_jaxpr/ppermute | solution.py:60
  227.4 25.5 %collective-permute-start = (bf16[1,1024,4,256]{3,1,2,0:T(8,128)(2,1)}, bf16[1,1024,4,256]{3,1,2,0:T(8,128)(2,1)}, u32[]{:S(2)}, u32[]{:S(2)}) collective-permute-start(bf16[1,1024,4,256]{3,1,2,0:T(8,128)(2,1)} %get-tuple-element.612), channel_id=1, source_target_pairs={{0,1},{1,2},{2,3},{3,4},{4,5},{5,6},{6,7},{7,0},{8,9},{9,10},{10,1... | collective-permute-start | bytes 6291464 | tf_op jit(solution)/shard_map/while/body/eval_jaxpr/ppermute | solution.py:60
  230.0 57.7 %collective-permute-start.1 = (bf16[1,1024,4,256]{3,1,2,0:T(8,128)(2,1)}, bf16[1,1024,4,256]{3,1,2,0:T(8,128)(2,1)S(1)}, u32[]{:S(2)}, u32[]{:S(2)}) collective-permute-start(bf16[1,1024,4,256]{3,1,2,0:T(8,128)(2,1)} %get-tuple-element.613), channel_id=1, source_target_pairs={{0,1},{1,2},{2,3},{3,4},{4,5},{5,6},{6,7},{7,0},{8,9},{9,10},{10,1... | collective-permute-start | bytes 6291464 | tf_op jit(solution)/shard_map/while/body/eval_jaxpr/ppermute | solution.py:60
  307.2 25.5 %collective-permute-start = (bf16[1,1024,4,256]{3,1,2,0:T(8,128)(2,1)}, bf16[1,1024,4,256]{3,1,2,0:T(8,128)(2,1)}, u32[]{:S(2)}, u32[]{:S(2)}) collective-permute-start(bf16[1,1024,4,256]{3,1,2,0:T(8,128)(2,1)} %get-tuple-element.612), channel_id=1, source_target_pairs={{0,1},{1,2},{2,3},{3,4},{4,5},{5,6},{6,7},{7,0},{8,9},{9,10},{10,1... | collective-permute-start | bytes 6291464 | tf_op jit(solution)/shard_map/while/body/eval_jaxpr/ppermute | solution.py:60
  309.7 57.7 %collective-permute-start.1 = (bf16[1,1024,4,256]{3,1,2,0:T(8,128)(2,1)}, bf16[1,1024,4,256]{3,1,2,0:T(8,128)(2,1)S(1)}, u32[]{:S(2)}, u32[]{:S(2)}) collective-permute-start(bf16[1,1024,4,256]{3,1,2,0:T(8,128)(2,1)} %get-tuple-element.613), channel_id=1, source_target_pairs={{0,1},{1,2},{2,3},{3,4},{4,5},{5,6},{6,7},{7,0},{8,9},{9,10},{10,1... | collective-permute-start | bytes 6291464 | tf_op jit(solution)/shard_map/while/body/eval_jaxpr/ppermute | solution.py:60
  471.3 25.5 %collective-permute-start.2 = (bf16[1,1024,4,256]{3,1,2,0:T(8,128)(2,1)}, bf16[1,1024,4,256]{3,1,2,0:T(8,128)(2,1)S(1)}, u32[]{:S(2)}, u32[]{:S(2)}) collective-permute-start(bf16[1,1024,4,256]{3,1,2,0:T(8,128)(2,1)} %get-tuple-element.645), channel_id=1, source_target_pairs={{0,1},{1,2},{2,3},{3,4},{4,5},{5,6},{6,7},{7,0},{8,9},{9,10},{10,1... | collective-permute-start | bytes 6291464 | tf_op jit(solution)/shard_map/while/body/eval_jaxpr/ppermute | solution.py:72
  473.9 45.4 %collective-permute-start.3 = (bf16[1,1024,4,256]{3,1,2,0:T(8,128)(2,1)}, bf16[1,1024,4,256]{3,1,2,0:T(8,128)(2,1)}, u32[]{:S(2)}, u32[]{:S(2)}) collective-permute-start(bf16[1,1024,4,256]{3,1,2,0:T(8,128)(2,1)} %get-tuple-element.646), channel_id=1, source_target_pairs={{0,1},{1,2},{2,3},{3,4},{4,5},{5,6},{6,7},{7,0},{8,9},{9,10},{10,1... | collective-permute-start | bytes 6291464 | tf_op jit(solution)/shard_map/while/body/eval_jaxpr/ppermute | solution.py:72
  473.9 90.3 %collective-permute-start.4 = (f32[1,1024,4,256]{3,1,2,0:T(8,128)}, f32[1,1024,4,256]{3,1,2,0:T(8,128)}, u32[]{:S(2)}, u32[]{:S(2)}) collective-permute-start(f32[1,1024,4,256]{3,1,2,0:T(8,128)} %get-tuple-element.647), channel_id=1, source_target_pairs={{0,1},{1,2},{2,3},{3,4},{4,5},{5,6},{6,7},{7,0},{8,9},{9,10},{10,1... | collective-permute-start | bytes 12582920 | tf_op jit(solution)/shard_map/while/body/eval_jaxpr/ppermute | solution.py:72
  475.6 133.6 %collective-permute-start.5 = (f32[1,1024,4,256]{3,1,2,0:T(8,128)}, f32[1,1024,4,256]{3,1,2,0:T(8,128)}, u32[]{:S(2)}, u32[]{:S(2)}) collective-permute-start(f32[1,1024,4,256]{3,1,2,0:T(8,128)} %get-tuple-element.648), channel_id=1, source_target_pairs={{0,1},{1,2},{2,3},{3,4},{4,5},{5,6},{6,7},{7,0},{8,9},{9,10},{10,1... | collective-permute-start | bytes 12582920 | tf_op jit(solution)/shard_map/while/body/eval_jaxpr/ppermute | solution.py:72
  627.8 25.5 %collective-permute-start.2 = (bf16[1,1024,4,256]{3,1,2,0:T(8,128)(2,1)}, bf16[1,1024,4,256]{3,1,2,0:T(8,128)(2,1)S(1)}, u32[]{:S(2)}, u32[]{:S(2)}) collective-permute-start(bf16[1,1024,4,256]{3,1,2,0:T(8,128)(2,1)} %get-tuple-element.645), channel_id=1, source_target_pairs={{0,1},{1,2},{2,3},{3,4},{4,5},{5,6},{6,7},{7,0},{8,9},{9,10},{10,1... | collective-permute-start | bytes 6291464 | tf_op jit(solution)/shard_map/while/body/eval_jaxpr/ppermute | solution.py:72
  630.3 45.4 %collective-permute-start.3 = (bf16[1,1024,4,256]{3,1,2,0:T(8,128)(2,1)}, bf16[1,1024,4,256]{3,1,2,0:T(8,128)(2,1)}, u32[]{:S(2)}, u32[]{:S(2)}) collective-permute-start(bf16[1,1024,4,256]{3,1,2,0:T(8,128)(2,1)} %get-tuple-element.646), channel_id=1, source_target_pairs={{0,1},{1,2},{2,3},{3,4},{4,5},{5,6},{6,7},{7,0},{8,9},{9,10},{10,1... | collective-permute-start | bytes 6291464 | tf_op jit(solution)/shard_map/while/body/eval_jaxpr/ppermute | solution.py:72
  630.4 90.3 %collective-permute-start.4 = (f32[1,1024,4,256]{3,1,2,0:T(8,128)}, f32[1,1024,4,256]{3,1,2,0:T(8,128)}, u32[]{:S(2)}, u32[]{:S(2)}) collective-permute-start(f32[1,1024,4,256]{3,1,2,0:T(8,128)} %get-tuple-element.647), channel_id=1, source_target_pairs={{0,1},{1,2},{2,3},{3,4},{4,5},{5,6},{6,7},{7,0},{8,9},{9,10},{10,1... | collective-permute-start | bytes 12582920 | tf_op jit(solution)/shard_map/while/body/eval_jaxpr/ppermute | solution.py:72
  632.1 133.6 %collective-permute-start.5 = (f32[1,1024,4,256]{3,1,2,0:T(8,128)}, f32[1,1024,4,256]{3,1,2,0:T(8,128)}, u32[]{:S(2)}, u32[]{:S(2)}) collective-permute-start(f32[1,1024,4,256]{3,1,2,0:T(8,128)} %get-tuple-element.648), channel_id=1, source_target_pairs={{0,1},{1,2},{2,3},{3,4},{4,5},{5,6},{6,7},{7,0},{8,9},{9,10},{10,1... | collective-permute-start | bytes 12582920 | tf_op jit(solution)/shard_map/while/body/eval_jaxpr/ppermute | solution.py:72
  786.8 45.4 %collective-permute-start.3 = (bf16[1,1024,4,256]{3,1,2,0:T(8,128)(2,1)}, bf16[1,1024,4,256]{3,1,2,0:T(8,128)(2,1)}, u32[]{:S(2)}, u32[]{:S(2)}) collective-permute-start(bf16[1,1024,4,256]{3,1,2,0:T(8,128)(2,1)} %get-tuple-element.646), channel_id=1, source_target_pairs={{0,1},{1,2},{2,3},{3,4},{4,5},{5,6},{6,7},{7,0},{8,9},{9,10},{10,1... | collective-permute-start | bytes 6291464 | tf_op jit(solution)/shard_map/while/body/eval_jaxpr/ppermute | solution.py:72
  786.8 90.3 %collective-permute-start.4 = (f32[1,1024,4,256]{3,1,2,0:T(8,128)}, f32[1,1024,4,256]{3,1,2,0:T(8,128)}, u32[]{:S(2)}, u32[]{:S(2)}) collective-permute-start(f32[1,1024,4,256]{3,1,2,0:T(8,128)} %get-tuple-element.647), channel_id=1, source_target_pairs={{0,1},{1,2},{2,3},{3,4},{4,5},{5,6},{6,7},{7,0},{8,9},{9,10},{10,1... | collective-permute-start | bytes 12582920 | tf_op jit(solution)/shard_map/while/body/eval_jaxpr/ppermute | solution.py:72
  788.6 133.6 %collective-permute-start.5 = (f32[1,1024,4,256]{3,1,2,0:T(8,128)}, f32[1,1024,4,256]{3,1,2,0:T(8,128)}, u32[]{:S(2)}, u32[]{:S(2)}) collective-permute-start(f32[1,1024,4,256]{3,1,2,0:T(8,128)} %get-tuple-element.648), channel_id=1, source_target_pairs={{0,1},{1,2},{2,3},{3,4},{4,5},{5,6},{6,7},{7,0},{8,9},{9,10},{10,1... | collective-permute-start | bytes 12582920 | tf_op jit(solution)/shard_map/while/body/eval_jaxpr/ppermute | solution.py:72
  940.8 25.5 %collective-permute-start.2 = (bf16[1,1024,4,256]{3,1,2,0:T(8,128)(2,1)}, bf16[1,1024,4,256]{3,1,2,0:T(8,128)(2,1)S(1)}, u32[]{:S(2)}, u32[]{:S(2)}) collective-permute-start(bf16[1,1024,4,256]{3,1,2,0:T(8,128)(2,1)} %get-tuple-element.645), channel_id=1, source_target_pairs={{0,1},{1,2},{2,3},{3,4},{4,5},{5,6},{6,7},{7,0},{8,9},{9,10},{10,1... | collective-permute-start | bytes 6291464 | tf_op jit(solution)/shard_map/while/body/eval_jaxpr/ppermute | solution.py:72
  943.3 45.4 %collective-permute-start.3 = (bf16[1,1024,4,256]{3,1,2,0:T(8,128)(2,1)}, bf16[1,1024,4,256]{3,1,2,0:T(8,128)(2,1)}, u32[]{:S(2)}, u32[]{:S(2)}) collective-permute-start(bf16[1,1024,4,256]{3,1,2,0:T(8,128)(2,1)} %get-tuple-element.646), channel_id=1, source_target_pairs={{0,1},{1,2},{2,3},{3,4},{4,5},{5,6},{6,7},{7,0},{8,9},{9,10},{10,1... | collective-permute-start | bytes 6291464 | tf_op jit(solution)/shard_map/while/body/eval_jaxpr/ppermute | solution.py:72
  943.3 90.3 %collective-permute-start.4 = (f32[1,1024,4,256]{3,1,2,0:T(8,128)}, f32[1,1024,4,256]{3,1,2,0:T(8,128)}, u32[]{:S(2)}, u32[]{:S(2)}) collective-permute-start(f32[1,1024,4,256]{3,1,2,0:T(8,128)} %get-tuple-element.647), channel_id=1, source_target_pairs={{0,1},{1,2},{2,3},{3,4},{4,5},{5,6},{6,7},{7,0},{8,9},{9,10},{10,1... | collective-permute-start | bytes 12582920 | tf_op jit(solution)/shard_map/while/body/eval_jaxpr/ppermute | solution.py:72
  945.0 133.6 %collective-permute-start.5 = (f32[1,1024,4,256]{3,1,2,0:T(8,128)}, f32[1,1024,4,256]{3,1,2,0:T(8,128)}, u32[]{:S(2)}, u32[]{:S(2)}) collective-permute-start(f32[1,1024,4,256]{3,1,2,0:T(8,128)} %get-tuple-element.648), channel_id=1, source_target_pairs={{0,1},{1,2},{2,3},{3,4},{4,5},{5,6},{6,7},{7,0},{8,9},{9,10},{10,1... | collective-permute-start | bytes 12582920 | tf_op jit(solution)/shard_map/while/body/eval_jaxpr/ppermute | solution.py:72
  1102.5 40.1 %collective-permute-start.6 = (bf16[1,1024,4,256]{3,2,1,0:T(4,128)(2,1)S(1)}, bf16[1,1024,4,256]{3,2,1,0:T(4,128)(2,1)}, u32[]{:S(2)}, u32[]{:S(2)}) collective-permute-start(bf16[1,1024,4,256]{3,2,1,0:T(4,128)(2,1)S(1)} %copy.28), channel_id=1, source_target_pairs={{0,4},{1,5},{2,6},{3,7},{4,0},{5,1},{6,2},{7,3},{8,12},{9,13},{10,... | collective-permute-start | bytes 6291464 | tf_op jit(solution)/shard_map/ppermute | solution.py:78
  1110.2 77.3 %collective-permute-start.7 = (bf16[1,1024,4,256]{3,2,1,0:T(4,128)(2,1)S(1)}, bf16[1,1024,4,256]{3,2,1,0:T(4,128)(2,1)}, u32[]{:S(2)}, u32[]{:S(2)}) collective-permute-start(bf16[1,1024,4,256]{3,2,1,0:T(4,128)(2,1)S(1)} %copy.29), channel_id=1, source_target_pairs={{0,4},{1,5},{2,6},{3,7},{4,0},{5,1},{6,2},{7,3},{8,12},{9,13},{10,... | collective-permute-start | bytes 6291464 | tf_op jit(solution)/shard_map/ppermute | solution.py:78
  (27 other events, 682.7 us)
where the time goes:
time: 1210 us; the launch traced here: 1200 us
  matrix products  567 us (47%)
  waiting for transfers between devices  395 us (33%)
  other arithmetic  105 us (9%)
  local copies, waits for them, and re-layouts  94.5 us (8%)
  starting transfers between devices  30.6 us (3%)
    ppermute x16, waiting for transfers between devices, bwd_body(): k_blk, v_blk, dk_run, dv_run = lax.ppermute(travel, 'ctx', shift_perm)  242 us
    dot_general x5, matrix products, bwd_block(): jnp.einsum('bqhgd,bkhd->bhgqk', do_five, v_blk, preferred_element_type=jn...  121 us
    dot_general x5, matrix products, bwd_block(): jnp.einsum('bhgqk,bqhgd->bkhd', p_blk.astype(jnp.bfloat16), do_five, pref...  92.3 us
    ppermute x8, waiting for transfers between devices, fwd_body(): kv_blk = lax.ppermute(kv_blk, 'ctx', shift_perm)  86.1 us
    dot_general x5, matrix products, fwd_update(): jnp.einsum('bqhgd,bkhd->bhgqk', q_five, k_blk, preferred_element_type=jnp...  78.9 us
    dot_general x5, matrix products, fwd_update(): jnp.einsum('bhgqk,bkhd->bhgqd', p_blk.astype(jnp.bfloat16), v_blk, prefer...  78.1 us
    reduce_sum x5, other arithmetic, fwd_update(): l_new = rescale * l_run + jnp.sum(p_blk, axis=-1)  78 us
    dot_general x5, matrix products, bwd_block(): jnp.einsum('bhgqk,bqhgd->bkhd', d_score, q_five, preferred_element_type=j...  69.3 us
  transfers between devices with their start and end apart: 26, of which 22 were waited for; matrix products, arithmetic and copies ran while one was open for 38% of the time, Pallas kernels for 0%

commit v1 on v0

v1 whole, which is shorter than its diff:
```python
import functools
import math

import jax
import jax.numpy as jnp
from jax import lax
from jax.experimental import pallas as pl
from jax.experimental.pallas import tpu as pltpu
from jax.sharding import PartitionSpec as P

WINDOW = 4096
NEG_BIG = -1e30
BLK = 512


def dot_nn(a, b):
    return lax.dot_general(a, b, (((1,), (0,)), ((), ())), preferred_element_type=jnp.float32)


def dot_nt(a, b):
    return lax.dot_general(a, b, (((1,), (1,)), ((), ())), preferred_element_type=jnp.float32)


def attn_kernel(q_ref, do_ref, k_ref, v_ref, o_ref, dq_ref, dk_ref, dv_ref, kt_ref, acc_ref, m_ref, l_ref, lse_ref, dqt_ref):
    n_chip, n_grp, chunk, dim = q_ref.shape
    core = lax.rem(lax.axis_index('ctx'), 2)
    per = chunk // BLK
    win = WINDOW // BLK
    scale = dim ** -0.5
    coef = scale * math.log2(math.e)

    def kv_slot(kb):
        chk = kb // per
        side = lax.rem(chk + core, 2)
        rows = pl.ds(pl.multiple_of(lax.rem(kb, per) * BLK, BLK), BLK)
        return side, chk // 2, rows

    def two_heads(ref, m, rows):
        return jnp.concatenate([ref[m, h, rows, :] for h in range(n_grp)], axis=0)

    for side in range(2):
        def tr_body(m, carry):
            kt_ref[side, m] = jnp.transpose(k_ref[side, m])
            return carry
        lax.fori_loop(0, n_chip, tr_body, 0)

    def zero_body(m, carry):
        for side in range(2):
            dk_ref[side, m] = jnp.zeros((chunk, dim), jnp.float32)
            dv_ref[side, m] = jnp.zeros((chunk, dim), jnp.float32)
        return carry
    lax.fori_loop(0, n_chip, zero_body, 0)

    tok_q = lax.rem(lax.broadcasted_iota(jnp.int32, (n_grp * BLK, BLK), 0), BLK)
    tok_k = lax.broadcasted_iota(jnp.int32, (n_grp * BLK, BLK), 1)
    tok_qt = lax.rem(lax.broadcasted_iota(jnp.int32, (BLK, n_grp * BLK), 1), BLK)
    tok_kt = lax.broadcasted_iota(jnp.int32, (BLK, n_grp * BLK), 0)

    def q_body(step, carry):
        m = step // per
        t = lax.rem(step, per)
        rows = pl.ds(pl.multiple_of(t * BLK, BLK), BLK)
        blk = (2 * m + core) * per + t
        lo = jnp.maximum(blk - win + 1, 0)

        def fwd(kb, kind):
            side, mk, krows = kv_slot(kb)
            s = dot_nt(two_heads(q_ref, m, rows), k_ref[side, mk, krows, :])
            if kind == 'diag':
                s = jnp.where(tok_k <= tok_q, s, NEG_BIG)
            elif kind == 'far':
                s = jnp.where(tok_k > tok_q, s, NEG_BIG)
            s_max = jnp.max(s, axis=1, keepdims=True)
            if kind == 'diag':
                m_new = jnp.broadcast_to(s_max, (n_grp * BLK, 128))
            else:
                m_old = m_ref[...]
                m_new = jnp.maximum(m_old, s_max)
                alpha = jnp.exp2((m_old - m_new) * coef)
            p = jnp.exp2(s * coef - (m_new * coef)[:, :1])
            p_sum = jnp.sum(p, axis=1, keepdims=True)
            pv = dot_nn(p.astype(jnp.bfloat16), v_ref[side, mk, krows, :])
            m_ref[...] = m_new
            if kind == 'diag':
                l_ref[...] = jnp.broadcast_to(p_sum, (n_grp * BLK, 128))
                acc_ref[...] = pv
            else:
                l_ref[...] = l_ref[...] * alpha + p_sum
                acc_ref[...] = acc_ref[...] * alpha[:, :1] + pv

        fwd(blk, 'diag')
        lax.fori_loop(lo, blk, lambda kb, c: (fwd(kb, 'full'), c)[1], 0)
        pl.when(blk >= win)(lambda: fwd(blk - win, 'far'))

        l_tot = l_ref[...]
        o = (acc_ref[...] * (1.0 / l_tot)[:, :1]).astype(jnp.bfloat16)
        for h in range(n_grp):
            o_ref[m, h, rows, :] = o[h * BLK:(h + 1) * BLK]
        lse_ref[0:1, :] = jnp.transpose(m_ref[...] * coef + jnp.log2(l_tot))[0:1, :]
        drow = jnp.sum(two_heads(do_ref, m, rows).astype(jnp.float32) * o.astype(jnp.float32), axis=1, keepdims=True)
        lse_ref[1:2, :] = jnp.transpose(jnp.broadcast_to(drow, (n_grp * BLK, 128)))[0:1, :]

        def bwd(kb, kind):
            side, mk, krows = kv_slot(kb)
            q2 = two_heads(q_ref, m, rows)
            do2 = two_heads(do_ref, m, rows)
            st = dot_nt(k_ref[side, mk, krows, :], q2)
            if kind == 'diag':
                st = jnp.where(tok_kt <= tok_qt, st, NEG_BIG)
            elif kind == 'far':
                st = jnp.where(tok_kt > tok_qt, st, NEG_BIG)
            dpt = dot_nt(v_ref[side, mk, krows, :], do2)
            p = jnp.exp2(st * coef - lse_ref[0:1, :])
            ds = (p * (dpt - lse_ref[1:2, :])).astype(jnp.bfloat16)
            dv_ref[side, mk, krows, :] += dot_nn(p.astype(jnp.bfloat16), do2)
            dk_ref[side, mk, krows, :] += dot_nn(ds, q2)
            dqt = dot_nn(kt_ref[side, mk, :, krows], ds)
            if kind == 'diag':
                dqt_ref[...] = dqt
            else:
                dqt_ref[...] += dqt

        bwd(blk, 'diag')
        lax.fori_loop(lo, blk, lambda kb, c: (bwd(kb, 'full'), c)[1], 0)
        pl.when(blk >= win)(lambda: bwd(blk - win, 'far'))
        dq = jnp.transpose(dqt_ref[...] * scale).astype(jnp.bfloat16)
        for h in range(n_grp):
            dq_ref[m, h, rows, :] = dq[h * BLK:(h + 1) * BLK]
        return carry

    lax.fori_loop(0, n_chip * per, q_body, 0)

    def scale_body(m, carry):
        for side in range(2):
            dk_ref[side, m] *= scale
        return carry
    lax.fori_loop(0, n_chip, scale_body, 0)


def solution(mesh):
    n_ctx = mesh.shape['ctx']
    n_chip = n_ctx // 2
    seq_spec = P('dp', 'ctx', None, None)
    groups = [[2 * x + c for x in range(n_chip)] for c in range(2)]
    swap = [(j, j ^ 1) for j in range(n_ctx)]

    def a2a(x):
        return lax.all_to_all(x, 'ctx', 0, 0, axis_index_groups=groups, tiled=True)

    def local_attn(q_loc, k_loc, v_loc, do_loc):
        _, chunk, q_heads, dim = q_loc.shape
        kv_heads = k_loc.shape[2]
        n_grp = q_heads // kv_heads

        def spread_q(x):
            return a2a(jnp.transpose(x.reshape(chunk, kv_heads, n_grp, dim), (1, 2, 0, 3)))

        def spread_kv(x):
            own = a2a(jnp.transpose(x.reshape(chunk, kv_heads, dim), (1, 0, 2)))
            return jnp.stack([own, lax.ppermute(own, 'ctx', swap)])

        k_all, v_all, q_all, do_all = spread_kv(k_loc), spread_kv(v_loc), spread_q(q_loc), spread_q(do_loc)
        q_type = jax.ShapeDtypeStruct((n_chip, n_grp, chunk, dim), jnp.bfloat16)
        kv_type = jax.ShapeDtypeStruct((2, n_chip, chunk, dim), jnp.float32)
        rows = n_grp * BLK
        o_all, dq_all, dk_all, dv_all = pl.pallas_call(
            attn_kernel,
            out_shape=(q_type, q_type, kv_type, kv_type),
            in_specs=[pl.BlockSpec(memory_space=pltpu.VMEM)] * 4,
            out_specs=[pl.BlockSpec(memory_space=pltpu.VMEM)] * 4,
            scratch_shapes=[
                pltpu.VMEM((2, n_chip, dim, chunk), jnp.bfloat16),
                pltpu.VMEM((rows, dim), jnp.float32),
                pltpu.VMEM((rows, 128), jnp.float32),
                pltpu.VMEM((rows, 128), jnp.float32),
                pltpu.VMEM((8, rows), jnp.float32),
                pltpu.VMEM((dim, rows), jnp.float32),
            ],
            compiler_params=pltpu.CompilerParams(vmem_limit_bytes=64000 * 1024),
        )(q_all, do_all, k_all, v_all)

        def home_q(x):
            return jnp.transpose(a2a(x), (2, 0, 1, 3)).reshape(q_loc.shape)

        def home_kv(x):
            total = (x[0] + lax.ppermute(x[1], 'ctx', swap)).astype(jnp.bfloat16)
            return jnp.transpose(a2a(total), (1, 0, 2)).reshape(k_loc.shape)

        return home_q(o_all), home_q(dq_all), home_kv(dk_all), home_kv(dv_all)

    return jax.shard_map(local_attn, mesh=mesh, in_specs=(seq_spec,) * 4, out_specs=(seq_spec,) * 4, check_vma=False)
```

time: 1210 us -> 544 us (0.45); the launches traced: 1200 us -> 543 us
  matrix products: 567 us -> 0 us
  Pallas kernels: 0 us -> 243 us
  waiting for transfers between devices: 395 us -> 194 us
  other arithmetic: 105 us -> 16.8 us
  local copies, waits for them, and re-layouts: 94.5 us -> 46.2 us
    dot_general x34 -> x0, matrix products: 567 us -> none  [the longest x5 121 us: bwd_block(): jnp.einsum('bqhgd,bkhd->bhgqk', do_five, v_blk, preferred_element_type=jn...]
    ppermute x26 -> x4, waiting for transfers between devices: 395 us -> 3.7 us  [the longest x2 3.69 us: spread_kv(): return jnp.stack([own, lax.ppermute(own, 'ctx', swap)])]
    pallas_call x0 -> x1, Pallas kernels: none -> 243 us  [local_attn(): pl.pallas_call(attn_kernel, out_shape=(q_type, q_type, kv_type, kv_type),...]
    all_to_all x0 -> x8, waiting for transfers between devices: none -> 190 us  [a2a(): return lax.all_to_all(x, 'ctx', 0, 0, axis_index_groups=groups, tiled=True)]
    reduce_sum x5 -> x0, other arithmetic: 78 us -> none  [fwd_update(): l_new = rescale * l_run + jnp.sum(p_blk, axis=-1)]
    while x46 -> x0, local copies, waits for them, and re-layouts: 57.9 us -> none
    all_to_all x0 -> x8, starting transfers between devices: none -> 38.2 us  [a2a(): return lax.all_to_all(x, 'ctx', 0, 0, axis_index_groups=groups, tiled=True)]
    ppermute x26 -> x4, starting transfers between devices: 30.6 us -> 4.08 us  [the longest x2 4.08 us: spread_kv(): return jnp.stack([own, lax.ppermute(own, 'ctx', swap)])]
  transfers between devices with their start and end apart: 26 -> 12, of which waited for: 22 -> 8; matrix products, arithmetic and copies ran while one was open for 38% -> 10% of each run, Pallas kernels for 0% -> 0%
where the time goes in v1:
time: 544 us; the launch traced here: 543 us
  Pallas kernels  243 us (45%)
  waiting for transfers between devices  194 us (36%)
  local copies, waits for them, and re-layouts  46.2 us (8%)
  starting transfers between devices  42.3 us (8%)
  other arithmetic  16.8 us (3%)
    pallas_call x1, Pallas kernels, local_attn(): pl.pallas_call(attn_kernel, out_shape=(q_type, q_type, kv_type, kv_type),...  243 us
    all_to_all x8, waiting for transfers between devices, a2a(): return lax.all_to_all(x, 'ctx', 0, 0, axis_index_groups=groups, tiled=True)  190 us
    all_to_all x8, starting transfers between devices, a2a(): return lax.all_to_all(x, 'ctx', 0, 0, axis_index_groups=groups, tiled=True)  38.2 us
    unnamed x8, local copies, waits for them, and re-layouts  37.1 us
  transfers between devices with their start and end apart: 12, of which 8 were waited for; matrix products, arithmetic and copies ran while one was open for 10% of the time, Pallas kernels for 0%

profile of v1, /device:TPU:113, one launch (start us, length us, event | category | flops | bytes accessed | tf_op | source)
XLA Modules:
  0.0 542.9 jit_solution(17468616645790604702)
XLA Ops:
  3.8 5.1 all-to-all-start.2
  12.1 22.2 %all-to-all-done.2 = bf16[4,1024,256]{2,1,0:T(8,128)(2,1)S(1)} async-done(((bf16[4,1024,256]{2,1,0:T(8,128)(2,1)}), bf16[4,1024,256]{2,1,0:T(8,128)(2,1)S(1)}, u32[]{:S(2)}, u32[]{:S(2)}) %all-to-all-start.2) | async-done | bytes 2097184 | tf_op jit(solution)/shard_map/all_to_all | solution.py:148
  34.3 4.5 all-to-all-start.3
  38.8 5.1 copy.8
  43.9 19.2 %all-to-all-done.3 = bf16[4,1024,256]{2,1,0:T(8,128)(2,1)} async-done(((bf16[4,1024,256]{2,1,0:T(8,128)(2,1)}), bf16[4,1024,256]{2,1,0:T(8,128)(2,1)}, u32[]{:S(2)}, u32[]{:S(2)}) %all-to-all-start.3) | async-done | bytes 2097184 | tf_op jit(solution)/shard_map/all_to_all | solution.py:148
  63.1 4.9 all-to-all-start
  68.0 5.1 copy.9
  73.1 40.7 %all-to-all-done.q_ref = bf16[4,2,1024,256]{3,2,1,0:T(8,128)(2,1)} async-done(((bf16[4,2,1024,256]{3,2,1,0:T(8,128)(2,1)}), bf16[4,2,1024,256]{3,2,1,0:T(8,128)(2,1)}, u32[]{:S(2)}, u32[]{:S(2)}) %all-to-all-start) | async-done | bytes 4194336 | tf_op jit(solution)/shard_map/all_to_all | solution.py:148
  113.8 5.2 all-to-all-start.1
  133.1 30.5 %all-to-all-done.1.do_ref = bf16[4,2,1024,256]{3,2,1,0:T(8,128)(2,1)} async-done(((bf16[4,2,1024,256]{3,2,1,0:T(8,128)(2,1)}), bf16[4,2,1024,256]{3,2,1,0:T(8,128)(2,1)}, u32[]{:S(2)}, u32[]{:S(2)}) %all-to-all-start.1) | async-done | bytes 4194336 | tf_op jit(solution)/shard_map/all_to_all | solution.py:148
  163.6 242.9 %shard_map.75 = (bf16[4,2,1024,256]{3,2,1,0:T(8,128)(2,1)}, bf16[4,2,1024,256]{3,2,1,0:T(8,128)(2,1)}, f32[2,4,1024,256]{3,2,1,0:T(8,128)}, f32[2,4,1024,256]{3,2,1,0:T(8,128)}) custom-call(bf16[4,2,1024,256]{3,2,1,0:T(8,128)(2,1)} %all-to-all-done.q_ref, bf16[4,2,1024,256]{3,2,1,0:T(8,128)(2,1)} %all-to-all-done.1.do_ref, ...), custom_call_target="tpu_custom_call" | custom-call | tf_op jit(solution)/shard_map/pallas_call | solution.py:166
  406.5 4.9 all-to-all-start.4
  411.4 4.5 slice_bitcast_fusion
  415.9 34.1 %all-to-all-done.4 = bf16[4,2,1024,256]{3,2,1,0:T(8,128)(2,1)} async-done(((bf16[4,2,1024,256]{3,2,1,0:T(8,128)(2,1)}), bf16[4,2,1024,256]{3,2,1,0:T(8,128)(2,1)}, u32[]{:S(2)}, u32[]{:S(2)}) %all-to-all-start.4) | async-done | bytes 4194336 | tf_op jit(solution)/shard_map/all_to_all | solution.py:148
  450.0 5.2 all-to-all-start.5
  455.3 4.6 slice_bitcast_fusion.1
  459.9 5.2 fusion
  465.1 26.7 %all-to-all-done.5 = bf16[4,2,1024,256]{3,2,1,0:T(8,128)(2,1)} async-done(((bf16[4,2,1024,256]{3,2,1,0:T(8,128)(2,1)}), bf16[4,2,1024,256]{3,2,1,0:T(8,128)(2,1)}, u32[]{:S(2)}, u32[]{:S(2)}) %all-to-all-start.5) | async-done | bytes 4194336 | tf_op jit(solution)/shard_map/all_to_all | solution.py:148
  495.6 5.2 fusion.1
  500.8 16.9 %all-to-all-done.7 = bf16[4,1024,256]{2,1,0:T(8,128)(2,1)S(1)} async-done(((bf16[4,1024,256]{2,1,0:T(8,128)(2,1)}), bf16[4,1024,256]{2,1,0:T(8,128)(2,1)S(1)}, u32[]{:S(2)}, u32[]{:S(2)}) %all-to-all-start.7) | async-done | bytes 2097184 | tf_op jit(solution)/shard_map/all_to_all | solution.py:148
  517.7 4.5 all-to-all-start.6
  522.3 6.6 %copy.12 = bf16[1,1024,8,256]{3,2,1,0:T(8,128)(2,1)} copy(bf16[1,1024,8,256]{3,1,2,0:T(8,128)(2,1)} %bitcast.13) | data formatting | bytes 8388608
  528.8 6.6 %copy.13 = bf16[1,1024,8,256]{3,2,1,0:T(8,128)(2,1)} copy(bf16[1,1024,8,256]{3,1,2,0:T(8,128)(2,1)} %bitcast.15) | data formatting | bytes 8388608
  538.4 4.5 copy.14
  (15 shorter events, 27.1 us)
Async XLA Ops:
  3.8 30.5 %all-to-all-start.2 = ((bf16[4,1024,256]{2,1,0:T(8,128)(2,1)}), bf16[4,1024,256]{2,1,0:T(8,128)(2,1)S(1)}, u32[]{:S(2)}, u32[]{:S(2)}) async-start(bf16[4,1024,256]{2,1,0:T(8,128)(2,1)} %bitcast.43), calls=%async_computation.2 | async-start | bytes 4194304 | tf_op jit(solution)/shard_map/all_to_all | solution.py:148
  34.3 28.8 %all-to-all-start.3 = ((bf16[4,1024,256]{2,1,0:T(8,128)(2,1)}), bf16[4,1024,256]{2,1,0:T(8,128)(2,1)}, u32[]{:S(2)}, u32[]{:S(2)}) async-start(bf16[4,1024,256]{2,1,0:T(8,128)(2,1)} %bitcast.42), calls=%async_computation.3 | async-start | bytes 4194304 | tf_op jit(solution)/shard_map/all_to_all | solution.py:148
  63.1 50.7 %all-to-all-start = ((bf16[4,2,1024,256]{3,2,1,0:T(8,128)(2,1)}), bf16[4,2,1024,256]{3,2,1,0:T(8,128)(2,1)}, u32[]{:S(2)}, u32[]{:S(2)}) async-start(bf16[4,2,1024,256]{3,2,1,0:T(8,128)(2,1)} %bitcast.45), calls=%async_computation | async-start | bytes 8388608 | tf_op jit(solution)/shard_map/all_to_all | solution.py:148
  113.8 49.8 %all-to-all-start.1 = ((bf16[4,2,1024,256]{3,2,1,0:T(8,128)(2,1)}), bf16[4,2,1024,256]{3,2,1,0:T(8,128)(2,1)}, u32[]{:S(2)}, u32[]{:S(2)}) async-start(bf16[4,2,1024,256]{3,2,1,0:T(8,128)(2,1)} %bitcast.44), calls=%async_computation.1 | async-start | bytes 8388608 | tf_op jit(solution)/shard_map/all_to_all | solution.py:148
  119.0 7.8 %collective-permute-start.1 = (bf16[4,1024,256]{2,1,0:T(8,128)(2,1)}, bf16[4,1024,256]{2,1,0:T(8,128)(2,1)S(1)}, u32[]{:S(2)}, u32[]{:S(2)}) collective-permute-start(bf16[4,1024,256]{2,1,0:T(8,128)(2,1)} %all-to-all-done.3), channel_id=1, source_target_pairs={{0,1},{1,0},{2,3},{3,2},{4,5},{5,4},{6,7},{7,6},{8,9},{9,8},{10,11... | collective-permute-start | bytes 6291464 | tf_op jit(solution)/shard_map/ppermute | solution.py:160
  123.0 7.7 %collective-permute-start = (bf16[4,1024,256]{2,1,0:T(8,128)(2,1)S(1)}, bf16[4,1024,256]{2,1,0:T(8,128)(2,1)S(1)}, u32[]{:S(2)}, u32[]{:S(2)}) collective-permute-start(bf16[4,1024,256]{2,1,0:T(8,128)(2,1)S(1)} %all-to-all-done.2), channel_id=1, source_target_pairs={{0,1},{1,0},{2,3},{3,2},{4,5},{5,4},{6,7},{7,6},{8,9},{9,8},{10,11... | collective-permute-start | bytes 6291464 | tf_op jit(solution)/shard_map/ppermute | solution.py:160
  406.5 43.6 %all-to-all-start.4 = ((bf16[4,2,1024,256]{3,2,1,0:T(8,128)(2,1)}), bf16[4,2,1024,256]{3,2,1,0:T(8,128)(2,1)}, u32[]{:S(2)}, u32[]{:S(2)}) async-start(bf16[4,2,1024,256]{3,2,1,0:T(8,128)(2,1)} %get-tuple-element.8), calls=%async_computation.4 | async-start | bytes 8388608 | tf_op jit(solution)/shard_map/all_to_all | solution.py:148
  415.9 43.9 %collective-permute-start.3 = (f32[4,1024,256]{2,1,0:T(8,128)}, f32[4,1024,256]{2,1,0:T(8,128)}, u32[]{:S(2)}, u32[]{:S(2)}) collective-permute-start(f32[4,1024,256]{2,1,0:T(8,128)} %slice_bitcast_fusion), channel_id=1, source_target_pairs={{0,1},{1,0},{2,3},{3,2},{4,5},{5,4},{6,7},{7,6},{8,9},{9,8},{10,11... | collective-permute-start | bytes 12582920 | tf_op jit(solution)/shard_map/ppermute | solution.py:186
  450.0 41.8 %all-to-all-start.5 = ((bf16[4,2,1024,256]{3,2,1,0:T(8,128)(2,1)}), bf16[4,2,1024,256]{3,2,1,0:T(8,128)(2,1)}, u32[]{:S(2)}, u32[]{:S(2)}) async-start(bf16[4,2,1024,256]{3,2,1,0:T(8,128)(2,1)} %get-tuple-element.9), calls=%async_computation.5 | async-start | bytes 8388608 | tf_op jit(solution)/shard_map/all_to_all | solution.py:148
  459.8 35.7 %collective-permute-start.2 = (f32[4,1024,256]{2,1,0:T(8,128)}, f32[4,1024,256]{2,1,0:T(8,128)}, u32[]{:S(2)}, u32[]{:S(2)}) collective-permute-start(f32[4,1024,256]{2,1,0:T(8,128)} %slice_bitcast_fusion.1), channel_id=1, source_target_pairs={{0,1},{1,0},{2,3},{3,2},{4,5},{5,4},{6,7},{7,6},{8,9},{9,8},{10,11... | collective-permute-start | bytes 12582920 | tf_op jit(solution)/shard_map/ppermute | solution.py:186
  491.8 25.9 %all-to-all-start.7 = ((bf16[4,1024,256]{2,1,0:T(8,128)(2,1)}), bf16[4,1024,256]{2,1,0:T(8,128)(2,1)S(1)}, u32[]{:S(2)}, u32[]{:S(2)}) async-start(bf16[4,1024,256]{2,1,0:T(8,128)(2,1)} %fusion), calls=%async_computation.7 | async-start | bytes 4194304 | tf_op jit(solution)/shard_map/all_to_all | solution.py:148
  517.7 20.6 %all-to-all-start.6 = ((bf16[4,1024,256]{2,1,0:T(8,128)(2,1)}), bf16[4,1024,256]{2,1,0:T(8,128)(2,1)}, u32[]{:S(2)}, u32[]{:S(2)}) async-start(bf16[4,1024,256]{2,1,0:T(8,128)(2,1)} %fusion.1), calls=%async_computation.6 | async-start | bytes 4194304 | tf_op jit(solution)/shard_map/all_to_all | solution.py:148

commit v2 on v1

v2 whole, which is shorter than its diff:
```python
import math

import jax
import jax.numpy as jnp
from jax import lax
from jax.experimental import pallas as pl
from jax.experimental.pallas import tpu as pltpu
from jax.sharding import PartitionSpec as P

WINDOW = 4096
NEG_BIG = -1e30
MESH = pl.DeviceIdType.MESH
K, V, KX, VX, Q, DO, O, DQ, DK, DV, DKX, DVX = range(12)


def dot_nn(a, b):
    return lax.dot_general(a, b, (((1,), (0,)), ((), ())), preferred_element_type=jnp.float32)


def dot_nt(a, b):
    return lax.dot_general(a, b, (((1,), (1,)), ((), ())), preferred_element_type=jnp.float32)


def attn_kernel(q_in, do_in, k_in, v_in, o_out, dq_out, dk_out, dv_out,
                q_all, do_all, k_all, v_all, kt_all, dk_all, dv_all, o_all, dq_all, dkx, dvx,
                acc_ref, m_ref, l_ref, lse_ref, dqt_ref, send_sem, recv_sem):
    n_chip, n_half, n_grp, blk_len, dim = q_in.shape
    chunk = n_half * blk_len
    n_dev = 2 * n_chip
    rows2 = n_grp * blk_len
    me = lax.axis_index('ctx')
    chip, core = me // 2, lax.rem(me, 2)
    win = WINDOW // blk_len
    scale = dim ** -0.5
    coef = scale * math.log2(math.e)

    def order(i):
        return i + i // 2 - 2 * (i // 3)

    def ahead(s):
        return lax.rem(chip + s, n_chip)

    def behind(s):
        return lax.rem(chip + n_chip - s, n_chip)

    def remote(kind, idx, src, dst, to_chip, to_core):
        return pltpu.make_async_remote_copy(
            src_ref=src, dst_ref=dst, send_sem=send_sem.at[kind, idx], recv_sem=recv_sem.at[kind, idx],
            device_id={'ctx': 2 * to_chip + to_core}, device_id_type=MESH)

    def local(kind, idx, src, dst):
        return pltpu.make_async_copy(src, dst, recv_sem.at[kind, idx])

    barrier = pltpu.get_barrier_semaphore()
    for step in range(1, n_dev):
        pl.semaphore_signal(barrier, inc=1, device_id={'ctx': lax.rem(me + step, n_dev)}, device_id_type=MESH)
    pl.semaphore_wait(barrier, n_dev - 1)

    def send_kv(kind, s):
        src, dst = ((k_in, k_all), (v_in, v_all))[kind]
        return remote(kind, s, src.at[ahead(s)], dst.at[0, chip], ahead(s), core)

    def send_q(kind, s, t):
        src, dst = ((q_in, q_all), (do_in, do_all))[kind - Q]
        return remote(kind, 2 * s + t, src.at[ahead(s), t], dst.at[chip, t], ahead(s), lax.rem(core + t, 2))

    own_copies = (local(K, 0, k_in.at[chip], k_all.at[0, chip]), local(V, 0, v_in.at[chip], v_all.at[0, chip]),
                  local(Q, 0, q_in.at[chip, 0], q_all.at[chip, 0]), local(DO, 0, do_in.at[chip, 0], do_all.at[chip, 0]))
    sends = []
    for s in (1, 3, 2):
        sends += [send_kv(K, s), send_kv(V, s)]
    for pair in ((1, 3), (2,)):
        for kind in (Q, DO):
            sends += [send_q(kind, s, t) for s in pair for t in range(2)]
    sends += [send_q(Q, 0, 1), send_q(DO, 0, 1)]
    for copy in own_copies:
        copy.start()
    for copy in sends:
        copy.start()

    def zero_body(m, carry):
        for side in range(2):
            dk_all[side, m] = jnp.zeros((chunk, dim), jnp.float32)
            dv_all[side, m] = jnp.zeros((chunk, dim), jnp.float32)
        return carry
    lax.fori_loop(0, n_chip, zero_body, 0)

    def pass_on(kind, s):
        ref = (k_all, v_all)[kind - KX]
        return remote(kind, s, ref.at[0, behind(s)], ref.at[1, behind(s)], chip, 1 - core)

    def own_side(i, carry):
        s = order(i)
        m = behind(s)

        @pl.when(i == 0)
        def _():
            own_copies[0].wait()
            own_copies[1].wait()

        @pl.when(i > 0)
        def _():
            remote(K, s, k_in.at[0], k_all.at[0, m], chip, core).wait_recv()
            remote(V, s, v_in.at[0], v_all.at[0, m], chip, core).wait_recv()
        pass_on(KX, s).start()
        pass_on(VX, s).start()
        kt_all[0, m] = jnp.transpose(k_all[0, m])
        return carry
    lax.fori_loop(0, n_chip, own_side, 0)

    def other_side(i, carry):
        s = order(i)
        m = behind(s)
        pass_on(KX, s).wait_recv()
        pass_on(VX, s).wait_recv()
        kt_all[1, m] = jnp.transpose(k_all[1, m])
        return carry
    lax.fori_loop(0, n_chip, other_side, 0)

    def kv_slot(kb):
        chk = kb // n_half
        rows = pl.ds(pl.multiple_of(lax.rem(kb, n_half) * blk_len, blk_len), blk_len)
        return lax.rem(chk + core, 2), chk // 2, rows

    tok_q = lax.rem(lax.broadcasted_iota(jnp.int32, (rows2, blk_len), 0), blk_len)
    tok_k = lax.broadcasted_iota(jnp.int32, (rows2, blk_len), 1)
    tok_qt = lax.rem(lax.broadcasted_iota(jnp.int32, (blk_len, rows2), 1), blk_len)
    tok_kt = lax.broadcasted_iota(jnp.int32, (blk_len, rows2), 0)

    def q_body(step, carry):
        s = order(lax.rem(step // 2 + 1, n_chip))
        u = lax.rem(step, 2)
        m = behind(s)
        idx = 2 * s + u
        is_own = step == 2 * n_chip - 2

        @pl.when(is_own)
        def _():
            own_copies[2].wait()
            own_copies[3].wait()

        @pl.when(jnp.logical_not(is_own))
        def _():
            remote(Q, idx, q_in.at[0, 0], q_all.at[m, u], chip, core).wait_recv()
            remote(DO, idx, do_in.at[0, 0], do_all.at[m, u], chip, core).wait_recv()

        blk = 2 * n_half * m + 2 * core + u * (3 - 4 * core)
        lo = jnp.maximum(blk - win + 1, 0)

        def fwd(kb, kind):
            side, mk, krows = kv_slot(kb)
            sc = dot_nt(q_all[m, u].reshape(rows2, dim), k_all[side, mk, krows, :])
            if kind == 'diag':
                sc = jnp.where(tok_k <= tok_q, sc, NEG_BIG)
            elif kind == 'far':
                sc = jnp.where(tok_k > tok_q, sc, NEG_BIG)
            s_max = jnp.max(sc, axis=1, keepdims=True)
            if kind == 'diag':
                m_new = jnp.broadcast_to(s_max, (rows2, 128))
            else:
                m_old = m_ref[...]
                m_new = jnp.maximum(m_old, s_max)
                alpha = jnp.exp2((m_old - m_new) * coef)
            p = jnp.exp2(sc * coef - (m_new * coef)[:, :1])
            p_sum = jnp.sum(p, axis=1, keepdims=True)
            pv = dot_nn(p.astype(jnp.bfloat16), v_all[side, mk, krows, :])
            m_ref[...] = m_new
            if kind == 'diag':
                l_ref[...] = jnp.broadcast_to(p_sum, (rows2, 128))
                acc_ref[...] = pv
            else:
                l_ref[...] = l_ref[...] * alpha + p_sum
                acc_ref[...] = acc_ref[...] * alpha[:, :1] + pv

        fwd(blk, 'diag')
        lax.fori_loop(lo, blk, lambda kb, c: (fwd(kb, 'full'), c)[1], 0)
        pl.when(blk >= win)(lambda: fwd(blk - win, 'far'))

        l_tot = l_ref[...]
        o = (acc_ref[...] * (1.0 / l_tot)[:, :1]).astype(jnp.bfloat16)
        o_all[m, u] = o.reshape(n_grp, blk_len, dim)
        lse_ref[0:1, :] = jnp.transpose(m_ref[...] * coef + jnp.log2(l_tot))[0:1, :]
        drow = jnp.sum(do_all[m, u].reshape(rows2, dim).astype(jnp.float32) * o.astype(jnp.float32), axis=1, keepdims=True)
        lse_ref[1:2, :] = jnp.transpose(jnp.broadcast_to(drow, (rows2, 128)))[0:1, :]

        @pl.when(is_own)
        def _():
            local(O, 0, o_all.at[chip, 0], o_out.at[chip, 0]).start()

        @pl.when(jnp.logical_not(is_own))
        def _():
            remote(O, idx, o_all.at[m, u], o_out.at[chip, u], m, lax.rem(core + u, 2)).start()

        def bwd(kb, kind):
            side, mk, krows = kv_slot(kb)
            q2 = q_all[m, u].reshape(rows2, dim)
            do2 = do_all[m, u].reshape(rows2, dim)
            st = dot_nt(k_all[side, mk, krows, :], q2)
            if kind == 'diag':
                st = jnp.where(tok_kt <= tok_qt, st, NEG_BIG)
            elif kind == 'far':
                st = jnp.where(tok_kt > tok_qt, st, NEG_BIG)
            dpt = dot_nt(v_all[side, mk, krows, :], do2)
            p = jnp.exp2(st * coef - lse_ref[0:1, :])
            ds = (p * (dpt - lse_ref[1:2, :])).astype(jnp.bfloat16)
            dv_all[side, mk, krows, :] += dot_nn(p.astype(jnp.bfloat16), do2)
            dk_all[side, mk, krows, :] += dot_nn(ds, q2)
            dqt = dot_nn(kt_all[side, mk, :, krows], ds)
            if kind == 'diag':
                dqt_ref[...] = dqt
            else:
                dqt_ref[...] += dqt

        bwd(blk, 'diag')
        lax.fori_loop(lo, blk, lambda kb, c: (bwd(kb, 'full'), c)[1], 0)
        pl.when(blk >= win)(lambda: bwd(blk - win, 'far'))
        dq_all[m, u] = jnp.transpose(dqt_ref[...] * scale).astype(jnp.bfloat16).reshape(n_grp, blk_len, dim)

        @pl.when(is_own)
        def _():
            local(DQ, 0, dq_all.at[chip, 0], dq_out.at[chip, 0]).start()

        @pl.when(jnp.logical_not(is_own))
        def _():
            remote(DQ, idx, dq_all.at[m, u], dq_out.at[chip, u], m, lax.rem(core + u, 2)).start()
        return carry

    lax.fori_loop(0, 2 * n_chip, q_body, 0)

    def swap(kind, m):
        src, dst = ((dk_all, dkx), (dv_all, dvx))[kind - DKX]
        return remote(kind, m, src.at[1, m], dst.at[m], chip, 1 - core)

    def swap_body(i, carry):
        m = behind(order(lax.rem(i + 1, n_chip)))
        swap(DKX, m).start()
        swap(DVX, m).start()
        return carry
    lax.fori_loop(0, n_chip, swap_body, 0)

    for i in range(n_chip):
        s = (i + 1) + (i + 1) // 2 - 2 * ((i + 1) // 3) if i < n_chip - 1 else 0
        m = behind(s)
        pass_on(KX, s).wait_send()
        pass_on(VX, s).wait_send()
        for kind, part, other, buf, out, mul in ((DK, dk_all, dkx, k_all, dk_out, scale), (DV, dv_all, dvx, v_all, dv_out, 1.0)):
            swap(kind + 2, m).wait_recv()

            def add_body(r, carry):
                rows = pl.ds(pl.multiple_of(r * 256, 256), 256)
                buf[0, m, rows, :] = ((part[0, m, rows, :] + other[m, rows, :]) * mul).astype(jnp.bfloat16)
                return carry
            lax.fori_loop(0, chunk // 256, add_body, 0)
            if s == 0:
                local(kind, 0, buf.at[0, chip], out.at[chip]).start()
            else:
                remote(kind, s, buf.at[0, m], out.at[chip], m, core).start()

    for copy in sends:
        copy.wait_send()
    for s in range(n_chip):
        m = behind(s)
        h = ahead(s)
        swap(DKX, m).wait_send()
        swap(DVX, m).wait_send()
        for kind, buf, out in ((O, o_all, o_out), (DQ, dq_all, dq_out)):
            for t in range(2):
                if s == 0 and t == 0:
                    local(kind, 0, buf.at[chip, 0], out.at[chip, 0]).wait()
                else:
                    remote(kind, 2 * s + t, buf.at[m, t], out.at[chip, t], m, lax.rem(core + t, 2)).wait_send()
                    remote(kind, 2 * s + t, buf.at[m, t], out.at[h, t], m, core).wait_recv()
        for kind, buf, out in ((DK, k_all, dk_out), (DV, v_all, dv_out)):
            if s == 0:
                local(kind, 0, buf.at[0, chip], out.at[chip]).wait()
            else:
                remote(kind, s, buf.at[0, m], out.at[chip], m, core).wait_send()
                remote(kind, s, buf.at[0, m], out.at[h], m, core).wait_recv()


def solution(mesh):
    n_chip = mesh.shape['ctx'] // 2
    seq_spec = P('dp', 'ctx', None, None)

    def local_attn(q_loc, k_loc, v_loc, do_loc):
        _, chunk, q_heads, dim = q_loc.shape
        kv_heads = k_loc.shape[2]
        n_grp = q_heads // kv_heads
        blk_len = chunk // 2
        rows = n_grp * blk_len
        bf16, f32 = jnp.bfloat16, jnp.float32

        def split_q(x):
            return jnp.transpose(x.reshape(2, blk_len, kv_heads, n_grp, dim), (2, 0, 3, 1, 4))

        def split_kv(x):
            return jnp.transpose(x.reshape(chunk, kv_heads, dim), (1, 0, 2))

        q_shape, kv_shape = (n_chip, 2, n_grp, blk_len, dim), (n_chip, chunk, dim)
        q_type, kv_type = jax.ShapeDtypeStruct(q_shape, bf16), jax.ShapeDtypeStruct(kv_shape, bf16)
        o_all, dq_all, dk_all, dv_all = pl.pallas_call(
            attn_kernel,
            out_shape=(q_type, q_type, kv_type, kv_type),
            in_specs=[pl.BlockSpec(memory_space=pl.ANY)] * 4,
            out_specs=[pl.BlockSpec(memory_space=pl.ANY)] * 4,
            scratch_shapes=[
                pltpu.VMEM(q_shape, bf16),
                pltpu.VMEM(q_shape, bf16),
                pltpu.VMEM((2,) + kv_shape, bf16),
                pltpu.VMEM((2,) + kv_shape, bf16),
                pltpu.VMEM((2, n_chip, dim, chunk), bf16),
                pltpu.VMEM((2,) + kv_shape, f32),
                pltpu.VMEM((2,) + kv_shape, f32),
                pltpu.VMEM(q_shape, bf16),
                pltpu.VMEM(q_shape, bf16),
                pltpu.VMEM(kv_shape, f32),
                pltpu.VMEM(kv_shape, f32),
                pltpu.VMEM((rows, dim), f32),
                pltpu.VMEM((rows, 128), f32),
                pltpu.VMEM((rows, 128), f32),
                pltpu.VMEM((8, rows), f32),
                pltpu.VMEM((dim, rows), f32),
                pltpu.SemaphoreType.DMA((12, 8)),
                pltpu.SemaphoreType.DMA((12, 8)),
            ],
            compiler_params=pltpu.CompilerParams(vmem_limit_bytes=67043328, collective_id=0, has_side_effects=True),
        )(split_q(q_loc), split_q(do_loc), split_kv(k_loc), split_kv(v_loc))

        def join_q(x):
            return jnp.transpose(x, (1, 3, 0, 2, 4)).reshape(q_loc.shape)

        def join_kv(x):
            return jnp.transpose(x, (1, 0, 2)).reshape(k_loc.shape)

        return join_q(o_all), join_q(dq_all), join_kv(dk_all), join_kv(dv_all)

    return jax.shard_map(local_attn, mesh=mesh, in_specs=(seq_spec,) * 4, out_specs=(seq_spec,) * 4, check_vma=False)
```

time: 544 us -> 382 us (0.70)
  waiting for transfers between devices: 194 us -> 0 us
  Pallas kernels: 243 us -> 352 us
  starting transfers between devices: 42.3 us -> 0 us
  local copies, waits for them, and re-layouts: 46.2 us -> 28.5 us
  other arithmetic: 16.8 us -> 0 us
    all_to_all x8 -> x0, waiting for transfers between devices: 190 us -> none  [a2a(): return lax.all_to_all(x, 'ctx', 0, 0, axis_index_groups=groups, tiled=True)]
    pallas_call x1, Pallas kernels: 243 us -> 352 us  [local_attn(): pl.pallas_call(attn_kernel, out_shape=(q_type, q_type, kv_type, kv_type),...]
    all_to_all x8 -> x0, starting transfers between devices: 38.2 us -> none  [a2a(): return lax.all_to_all(x, 'ctx', 0, 0, axis_index_groups=groups, tiled=True)]
    unnamed x8 -> x18, local copies, waits for them, and re-layouts: 37.1 us -> 19.1 us
    convert_element_type x2 -> x0, other arithmetic: 10.5 us -> none  [home_kv(): total = (x[0] + lax.ppermute(x[1], 'ctx', swap)).astype(jnp.bfloat16)]
    transpose x0 -> x4, local copies, waits for them, and re-layouts: none -> 9.42 us  [the longest x1 4.03 us: split_q(): jnp.transpose(x.reshape(2, blk_len, kv_heads, n_grp, dim), (2, 0, 3, 1, 4))]
    squeeze x2 -> x0, local copies, waits for them, and re-layouts: 9.1 us -> none  [home_kv(): total = (x[0] + lax.ppermute(x[1], 'ctx', swap)).astype(jnp.bfloat16)]
    another operation x2 -> x0, other arithmetic: 6.29 us -> none  [spread_kv(): return jnp.stack([own, lax.ppermute(own, 'ctx', swap)])]
  transfers between devices with their start and end apart: 12 -> 0, of which waited for: 8 -> 0; matrix products, arithmetic and copies ran while one was open for 10% -> 0% of each run, Pallas kernels for 0% -> 0%
where the time goes in v2:
time: 382 us
  Pallas kernels  352 us (92%)
  local copies, waits for them, and re-layouts  28.5 us (7%)
    pallas_call x1, Pallas kernels, local_attn(): pl.pallas_call(attn_kernel, out_shape=(q_type, q_type, kv_type, kv_type),...  352 us
    unnamed x18, local copies, waits for them, and re-layouts  19.1 us

profile of v2, /device:TPU:113, one launch (start us, length us, event | category | flops | bytes accessed | tf_op | source)
XLA Modules:
  0.0 381.6 jit_solution(15518075370882789448)
XLA Ops:
  0.6 0.0 copy-start
  0.6 3.2 copy.12
  3.8 0.2 copy-done
  4.1 0.9 copy.14
  4.9 0.0 copy-start.4
  5.0 0.0 copy-start.5
  5.0 4.0 %copy_bitcast_fusion = (bf16[4,2,2,512,256]{4,3,2,1,0:T(8,128)(2,1)}, bf16[4,2,2,512,256]{4,3,2,1,0:T(8,128)(2,1)}) fusion(bf16[2,512,4,2,256]{4,1,0,3,2:T(8,128)(2,1)S(1)} %bitcast.27, bf16[2,512,4,2,256]{4,1,0,3,2:T(8,128)(2,1)S(1)} %bitcast.26), kind=kLoop, calls=%fused_computation | loop fusion | bytes 16777216 | tf_op jit(solution)/shard_map/transpose | solution.py:294
  9.0 0.0 copy-done.4
  9.0 0.0 copy-done.5
  9.0 2.6 copy_bitcast_fusion.2
  11.6 352.4 %shard_map.75 = (bf16[4,2,2,512,256]{4,3,2,1,0:T(8,128)(2,1)}, bf16[4,2,2,512,256]{4,3,2,1,0:T(8,128)(2,1)}, bf16[4,1024,256]{2,1,0:T(8,128)(2,1)}, bf16[4,1024,256]{2,1,0:T(8,128)(2,1)}) custom-call(bf16[4,2,2,512,256]{4,3,2,1,0:T(8,128)(2,1)} %get-tuple-element.21.q_in, bf16[4,2,2,512,256]{4,3,2,1,0:T(8,128)(2,1)} %get-tuple-element.20.do_in, ...), custom_call_target="tpu_custom_call" | custom-call | tf_op jit(solution)/shard_map/pallas_call | solution.py:301
  364.0 2.5 copy.18
  366.5 0.0 copy-start.1
  366.5 4.4 %copy.20 = bf16[1,1024,8,256]{3,2,1,0:T(8,128)(2,1)} copy(bf16[1,1024,8,256]{3,1,2,0:T(8,128)(2,1)S(1)} %bitcast.24) | data formatting | bytes 8388608
  370.9 0.0 copy-done.1
  370.9 0.4 copy.19
  371.3 0.0 copy-start.3
  371.3 4.4 %copy.21 = bf16[1,1024,8,256]{3,2,1,0:T(8,128)(2,1)} copy(bf16[1,1024,8,256]{3,1,2,0:T(8,128)(2,1)S(1)} %bitcast.25) | data formatting | bytes 8388608
  375.7 0.0 copy-done.3
  375.7 0.0 copy-start.2
  375.8 2.9 copy.22
  378.7 0.0 copy-done.2
  378.7 2.9 copy.23
Async XLA Ops:
  0.6 3.5 copy-start
  4.9 4.1 %copy-start.4 = (bf16[1,1024,4,256]{3,2,1,0:T(4,128)(2,1)S(1)}, bf16[1,1024,4,256]{3,2,1,0:T(4,128)(2,1)}, u32[]{:S(2)}) copy-start(bf16[1,1024,4,256]{3,2,1,0:T(4,128)(2,1)} %param.6) | copy-start | bytes 6291460
  5.0 4.0 %copy-start.5 = (bf16[1,1024,4,256]{3,2,1,0:T(4,128)(2,1)S(1)}, bf16[1,1024,4,256]{3,2,1,0:T(4,128)(2,1)}, u32[]{:S(2)}) copy-start(bf16[1,1024,4,256]{3,2,1,0:T(4,128)(2,1)} %param.5) | copy-start | bytes 6291460
  366.5 4.4 %copy-start.1 = (bf16[4,2,2,512,256]{4,3,2,1,0:T(8,128)(2,1)S(1)}, bf16[4,2,2,512,256]{4,3,2,1,0:T(8,128)(2,1)}, u32[]{:S(2)}) copy-start(bf16[4,2,2,512,256]{4,3,2,1,0:T(8,128)(2,1)} %get-tuple-element.9) | copy-start | bytes 12582916
  371.3 4.4 %copy-start.3 = (bf16[4,1024,256]{2,1,0:T(8,128)(2,1)S(1)}, bf16[4,1024,256]{2,1,0:T(8,128)(2,1)}, u32[]{:S(2)}) copy-start(bf16[4,1024,256]{2,1,0:T(8,128)(2,1)} %get-tuple-element.10) | copy-start | bytes 6291460
  375.7 2.9 copy-start.2

commit v3 on v2

--- a/solution.py
+++ b/solution.py
@@ -23,7 +23,7 @@
 
 def attn_kernel(q_in, do_in, k_in, v_in, o_out, dq_out, dk_out, dv_out,
                 q_all, do_all, k_all, v_all, kt_all, dk_all, dv_all, o_all, dq_all, dkx, dvx,
-                acc_ref, m_ref, l_ref, lse_ref, dqt_ref, send_sem, recv_sem):
+                acc_ref, m_ref, l_ref, stat_ref, dqt_ref, send_sem, recv_sem):
     n_chip, n_half, n_grp, blk_len, dim = q_in.shape
     chunk = n_half * blk_len
     n_dev = 2 * n_chip
@@ -127,25 +127,22 @@
     tok_qt = lax.rem(lax.broadcasted_iota(jnp.int32, (blk_len, rows2), 1), blk_len)
     tok_kt = lax.broadcasted_iota(jnp.int32, (blk_len, rows2), 0)
 
-    def q_body(step, carry):
-        s = order(lax.rem(step // 2 + 1, n_chip))
-        u = lax.rem(step, 2)
-        m = behind(s)
-        idx = 2 * s + u
-        is_own = step == 2 * n_chip - 2
+    def block_of(s, u):
+        return 2 * n_half * behind(s) + 2 * core + u * (3 - 4 * core)
+
+    def fwd_task(s, u):
+        m, idx = behind(s), 2 * s + u
+        is_own = idx == 0
 
         @pl.when(is_own)
         def _():
             own_copies[2].wait()
-            own_copies[3].wait()
 
         @pl.when(jnp.logical_not(is_own))
         def _():
             remote(Q, idx, q_in.at[0, 0], q_all.at[m, u], chip, core).wait_recv()
-            remote(DO, idx, do_in.at[0, 0], do_all.at[m, u], chip, core).wait_recv()
-
-        blk = 2 * n_half * m + 2 * core + u * (3 - 4 * core)
-        lo = jnp.maximum(blk - win + 1, 0)
+
+        blk = block_of(s, u)
 
         def fwd(kb, kind):
             side, mk, krows = kv_slot(kb)
@@ -173,23 +170,43 @@
                 acc_ref[...] = acc_ref[...] * alpha[:, :1] + pv
 
         fwd(blk, 'diag')
-        lax.fori_loop(lo, blk, lambda kb, c: (fwd(kb, 'full'), c)[1], 0)
+        lax.fori_loop(jnp.maximum(blk - win + 1, 0), blk, lambda kb, c: (fwd(kb, 'full'), c)[1], 0)
         pl.when(blk >= win)(lambda: fwd(blk - win, 'far'))
 
         l_tot = l_ref[...]
-        o = (acc_ref[...] * (1.0 / l_tot)[:, :1]).astype(jnp.bfloat16)
-        o_all[m, u] = o.reshape(n_grp, blk_len, dim)
-        lse_ref[0:1, :] = jnp.transpose(m_ref[...] * coef + jnp.log2(l_tot))[0:1, :]
-        drow = jnp.sum(do_all[m, u].reshape(rows2, dim).astype(jnp.float32) * o.astype(jnp.float32), axis=1, keepdims=True)
-        lse_ref[1:2, :] = jnp.transpose(jnp.broadcast_to(drow, (rows2, 128)))[0:1, :]
-
-        @pl.when(is_own)
-        def _():
-            local(O, 0, o_all.at[chip, 0], o_out.at[chip, 0]).start()
-
-        @pl.when(jnp.logical_not(is_own))
-        def _():
-            remote(O, idx, o_all.at[m, u], o_out.at[chip, u], m, lax.rem(core + u, 2)).start()
+        o_all[m, u] = (acc_ref[...] * (1.0 / l_tot)[:, :1]).astype(jnp.bfloat16).reshape(n_grp, blk_len, dim)
+        stat_ref[idx, 0:1, :] = jnp.transpose(m_ref[...] * coef + jnp.log2(l_tot))[0:1, :]
+        send_back(O, s, u)
+
+    def send_back(kind, s, u):
+        buf, out = ((o_all, o_out), (dq_all, dq_out))[kind - O]
+        m, idx = behind(s), 2 * s + u
+
+        @pl.when(idx == 0)
+        def _():
+            local(kind, 0, buf.at[chip, 0], out.at[chip, 0]).start()
+
+        @pl.when(idx > 0)
+        def _():
+            remote(kind, idx, buf.at[m, u], out.at[chip, u], m, lax.rem(core + u, 2)).start()
+
+    def bwd_unit(s, u, kv_chip, first, last):
+        m, idx = behind(s), 2 * s + u
+        blk = block_of(s, u)
+
+        @pl.when(first)
+        def _():
+            @pl.when(idx == 0)
+            def _():
+                own_copies[3].wait()
+
+            @pl.when(idx > 0)
+            def _():
+                remote(DO, idx, do_in.at[0, 0], do_all.at[m, u], chip, core).wait_recv()
+            both = do_all[m, u].reshape(rows2, dim).astype(jnp.float32) * o_all[m, u].reshape(rows2, dim).astype(jnp.float32)
+            drow = jnp.sum(both, axis=1, keepdims=True)
+            stat_ref[idx, 1:2, :] = jnp.transpose(jnp.broadcast_to(drow, (rows2, 128)))[0:1, :]
+            dqt_ref[u] = jnp.zeros((dim, rows2), jnp.float32)
 
         def bwd(kb, kind):
             side, mk, krows = kv_slot(kb)
@@ -201,68 +218,99 @@
             elif kind == 'far':
                 st = jnp.where(tok_kt > tok_qt, st, NEG_BIG)
             dpt = dot_nt(v_all[side, mk, krows, :], do2)
-            p = jnp.exp2(st * coef - lse_ref[0:1, :])
-            ds = (p * (dpt - lse_ref[1:2, :])).astype(jnp.bfloat16)
+            p = jnp.exp2(st * coef - stat_ref[idx, 0:1, :])
+            ds = (p * (dpt - stat_ref[idx, 1:2, :])).astype(jnp.bfloat16)
             dv_all[side, mk, krows, :] += dot_nn(p.astype(jnp.bfloat16), do2)
             dk_all[side, mk, krows, :] += dot_nn(ds, q2)
-            dqt = dot_nn(kt_all[side, mk, :, krows], ds)
-            if kind == 'diag':
-                dqt_ref[...] = dqt
-            else:
-                dqt_ref[...] += dqt
-
-        bwd(blk, 'diag')
-        lax.fori_loop(lo, blk, lambda kb, c: (bwd(kb, 'full'), c)[1], 0)
-        pl.when(blk >= win)(lambda: bwd(blk - win, 'far'))
-        dq_all[m, u] = jnp.transpose(dqt_ref[...] * scale).astype(jnp.bfloat16).reshape(n_grp, blk_len, dim)
-
-        @pl.when(is_own)
-        def _():
-            local(DQ, 0, dq_all.at[chip, 0], dq_out.at[chip, 0]).start()
-
-        @pl.when(jnp.logical_not(is_own))
-        def _():
-            remote(DQ, idx, dq_all.at[m, u], dq_out.at[chip, u], m, lax.rem(core + u, 2)).start()
-        return carry
-
-    lax.fori_loop(0, 2 * n_chip, q_body, 0)
-
-    def swap(kind, m):
+            dqt_ref[u] += dot_nn(kt_all[side, mk, :, krows], ds)
+
+        per_chip = 2 * n_half
+        pl.when(jnp.logical_and(blk >= win, (blk - win + per_chip) // per_chip == kv_chip + 1))(lambda: bwd(blk - win, 'far'))
+        lo = jnp.maximum(jnp.maximum(blk - win + 1, 0), per_chip * kv_chip)
+        hi = jnp.minimum(blk, per_chip * kv_chip + per_chip)
+        lax.fori_loop(lo, hi, lambda kb, c: (bwd(kb, 'full'), c)[1], 0)
+        pl.when(kv_chip == m)(lambda: bwd(blk, 'diag'))
+
+        @pl.when(last)
+        def _():
+            dq_all[m, u] = jnp.transpose(dqt_ref[u] * scale).astype(jnp.bfloat16).reshape(n_grp, blk_len, dim)
+            send_back(DQ, s, u)
+
+    def swap(kind, s):
         src, dst = ((dk_all, dkx), (dv_all, dvx))[kind - DKX]
-        return remote(kind, m, src.at[1, m], dst.at[m], chip, 1 - core)
-
-    def swap_body(i, carry):
-        m = behind(order(lax.rem(i + 1, n_chip)))
-        swap(DKX, m).start()
-        swap(DVX, m).start()
-        return carry
-    lax.fori_loop(0, n_chip, swap_body, 0)
-
-    for i in range(n_chip):
-        s = (i + 1) + (i + 1) // 2 - 2 * ((i + 1) // 3) if i < n_chip - 1 else 0
+        return remote(kind, s, src.at[1, behind(s)], dst.at[behind(s)], chip, 1 - core)
+
+    def swap_start(s):
+        swap(DKX, s).start()
+        swap(DVX, s).start()
+
+    def settle(s):
         m = behind(s)
-        pass_on(KX, s).wait_send()
-        pass_on(VX, s).wait_send()
         for kind, part, other, buf, out, mul in ((DK, dk_all, dkx, k_all, dk_out, scale), (DV, dv_all, dvx, v_all, dv_out, 1.0)):
-            swap(kind + 2, m).wait_recv()
+            swap(kind + 2, s).wait_recv()
+            pass_on(kind - DK + KX, s).wait_send()
 
             def add_body(r, carry):
                 rows = pl.ds(pl.multiple_of(r * 256, 256), 256)
                 buf[0, m, rows, :] = ((part[0, m, rows, :] + other[m, rows, :]) * mul).astype(jnp.bfloat16)
                 return carry
             lax.fori_loop(0, chunk // 256, add_body, 0)
-            if s == 0:
+
+            @pl.when(s == 0)
+            def _():
                 local(kind, 0, buf.at[0, chip], out.at[chip]).start()
-            else:
+
+            @pl.when(s > 0)
+            def _():
                 remote(kind, s, buf.at[0, m], out.at[chip], m, core).start()
+
+    n_span = WINDOW // (2 * chunk) + 1
+    n_task = 4 * n_chip
+
+    def task_body(step, carry):
+        task, half = step // 2, lax.rem(step, 2)
+        is_fwd = jnp.logical_or(task < 3, task == 5)
+        s = jnp.where(task < 3, order(task), jnp.where(task < 5, order(task - 2), jnp.where(task < 7, 2, 0)))
+        pl.when(is_fwd)(lambda: fwd_task(s, half))
+
+        @pl.when(jnp.logical_not(is_fwd))
+        def _():
+            own = s == 0
+
+            def unit_body(j, carry):
+                k = half * n_span + j
+                u = jnp.where(own, lax.rem(k, 2), half)
+                y = jnp.where(own, k // 2, j)
+
+                @pl.when(jnp.logical_and(own, k == 0))
+                def _():
+                    swap_start(n_chip - 1)
+
+                bwd_unit(s, u, behind(s) - n_span + 1 + y, y == 0, y == n_span - 1)
+
+                @pl.when(own)
+                def _():
+                    @pl.when(lax.rem(k, 2) == 1)
+                    def _():
+                        swap_start(n_span - 1 - y)
+
+                    @pl.when(lax.rem(k, 2) == 0)
+                    def _():
+                        settle(lax.rem(n_span - y, n_chip))
+                return carry
+            lax.fori_loop(0, n_span, unit_body, 0)
+        return carry
+
+    lax.fori_loop(0, n_task, task_body, 0)
+    settle(0)
 
     for copy in sends:
         copy.wait_send()
     for s in range(n_chip):
         m = behind(s)
         h = ahead(s)
-        swap(DKX, m).wait_send()
-        swap(DVX, m).wait_send()
+        swap(DKX, s).wait_send()
+        swap(DVX, s).wait_send()
         for kind, buf, out in ((O, o_all, o_out), (DQ, dq_all, dq_out)):
             for t in range(2):
                 if s == 0 and t == 0:
@@ -318,8 +366,8 @@
                 pltpu.VMEM((rows, dim), f32),
                 pltpu.VMEM((rows, 128), f32),
                 pltpu.VMEM((rows, 128), f32),
-                pltpu.VMEM((8, rows), f32),
-                pltpu.VMEM((dim, rows), f32),
+                pltpu.VMEM((2 * n_chip, 8, rows), f32),
+                pltpu.VMEM((2, dim, rows), f32),
                 pltpu.SemaphoreType.DMA((12, 8)),
                 pltpu.SemaphoreType.DMA((12, 8)),
             ],

time: 382 us -> 354 us (0.927)
  Pallas kernels: 352 us -> 325 us
    pallas_call x1, Pallas kernels: 352 us -> 325 us  [local_attn(): pl.pallas_call(attn_kernel, out_shape=(q_type, q_type, kv_type, kv_type),...]
where the time goes in v3:
time: 354 us
  Pallas kernels  325 us (92%)
  local copies, waits for them, and re-layouts  28.5 us (8%)
    pallas_call x1, Pallas kernels, local_attn(): pl.pallas_call(attn_kernel, out_shape=(q_type, q_type, kv_type, kv_type),...  325 us
    unnamed x18, local copies, waits for them, and re-layouts  19.1 us

profile of v3, /device:TPU:113, one launch (start us, length us, event | category | flops | bytes accessed | tf_op | source)
XLA Modules:
  0.0 353.9 jit_solution(2273297928503470991)
XLA Ops:
  0.6 0.0 copy-start
  0.6 3.2 copy.12
  3.8 0.2 copy-done
  4.1 0.9 copy.14
  4.9 0.0 copy-start.4
  5.0 0.0 copy-start.5
  5.0 4.0 %copy_bitcast_fusion = (bf16[4,2,2,512,256]{4,3,2,1,0:T(8,128)(2,1)}, bf16[4,2,2,512,256]{4,3,2,1,0:T(8,128)(2,1)}) fusion(bf16[2,512,4,2,256]{4,1,0,3,2:T(8,128)(2,1)S(1)} %bitcast.27, bf16[2,512,4,2,256]{4,1,0,3,2:T(8,128)(2,1)S(1)} %bitcast.26), kind=kLoop, calls=%fused_computation | loop fusion | bytes 16777216 | tf_op jit(solution)/shard_map/transpose | solution.py:342
  9.0 0.0 copy-done.4
  9.0 0.0 copy-done.5
  9.0 2.6 copy_bitcast_fusion.2
  11.6 324.7 %shard_map.75 = (bf16[4,2,2,512,256]{4,3,2,1,0:T(8,128)(2,1)}, bf16[4,2,2,512,256]{4,3,2,1,0:T(8,128)(2,1)}, bf16[4,1024,256]{2,1,0:T(8,128)(2,1)}, bf16[4,1024,256]{2,1,0:T(8,128)(2,1)}) custom-call(bf16[4,2,2,512,256]{4,3,2,1,0:T(8,128)(2,1)} %get-tuple-element.21.q_in, bf16[4,2,2,512,256]{4,3,2,1,0:T(8,128)(2,1)} %get-tuple-element.20.do_in, ...), custom_call_target="tpu_custom_call" | custom-call | tf_op jit(solution)/shard_map/pallas_call | solution.py:349
  336.3 2.5 copy.18
  338.7 0.0 copy-start.1
  338.8 4.4 %copy.20 = bf16[1,1024,8,256]{3,2,1,0:T(8,128)(2,1)} copy(bf16[1,1024,8,256]{3,1,2,0:T(8,128)(2,1)S(1)} %bitcast.24) | data formatting | bytes 8388608
  343.2 0.0 copy-done.1
  343.2 0.4 copy.19
  343.6 0.0 copy-start.3
  343.6 4.4 %copy.21 = bf16[1,1024,8,256]{3,2,1,0:T(8,128)(2,1)} copy(bf16[1,1024,8,256]{3,1,2,0:T(8,128)(2,1)S(1)} %bitcast.25) | data formatting | bytes 8388608
  348.0 0.0 copy-done.3
  348.0 0.0 copy-start.2
  348.0 2.9 copy.22
  351.0 0.0 copy-done.2
  351.0 2.9 copy.23
Async XLA Ops:
  0.6 3.5 copy-start
  4.9 4.1 %copy-start.4 = (bf16[1,1024,4,256]{3,2,1,0:T(4,128)(2,1)S(1)}, bf16[1,1024,4,256]{3,2,1,0:T(4,128)(2,1)}, u32[]{:S(2)}) copy-start(bf16[1,1024,4,256]{3,2,1,0:T(4,128)(2,1)} %param.6) | copy-start | bytes 6291460
  5.0 4.0 %copy-start.5 = (bf16[1,1024,4,256]{3,2,1,0:T(4,128)(2,1)S(1)}, bf16[1,1024,4,256]{3,2,1,0:T(4,128)(2,1)}, u32[]{:S(2)}) copy-start(bf16[1,1024,4,256]{3,2,1,0:T(4,128)(2,1)} %param.5) | copy-start | bytes 6291460
  338.7 4.4 %copy-start.1 = (bf16[4,2,2,512,256]{4,3,2,1,0:T(8,128)(2,1)S(1)}, bf16[4,2,2,512,256]{4,3,2,1,0:T(8,128)(2,1)}, u32[]{:S(2)}) copy-start(bf16[4,2,2,512,256]{4,3,2,1,0:T(8,128)(2,1)} %get-tuple-element.9) | copy-start | bytes 12582916
  343.6 4.4 %copy-start.3 = (bf16[4,1024,256]{2,1,0:T(8,128)(2,1)S(1)}, bf16[4,1024,256]{2,1,0:T(8,128)(2,1)}, u32[]{:S(2)}) copy-start(bf16[4,1024,256]{2,1,0:T(8,128)(2,1)} %get-tuple-element.10) | copy-start | bytes 6291460
  348.0 2.9 copy-start.2

commit v4 on v3

--- a/solution.py
+++ b/solution.py
@@ -9,6 +9,7 @@
 
 WINDOW = 4096
 NEG_BIG = -1e30
+COLS = 256
 MESH = pl.DeviceIdType.MESH
 K, V, KX, VX, Q, DO, O, DQ, DK, DV, DKX, DVX = range(12)
 
@@ -21,10 +22,14 @@
     return lax.dot_general(a, b, (((1,), (1,)), ((), ())), preferred_element_type=jnp.float32)
 
 
+def dot_tn(a, b):
+    return lax.dot_general(a, b, (((0,), (0,)), ((), ())), preferred_element_type=jnp.float32)
+
+
 def attn_kernel(q_in, do_in, k_in, v_in, o_out, dq_out, dk_out, dv_out,
                 q_all, do_all, k_all, v_all, kt_all, dk_all, dv_all, o_all, dq_all, dkx, dvx,
-                acc_ref, m_ref, l_ref, stat_ref, dqt_ref, send_sem, recv_sem):
-    n_chip, n_half, n_grp, blk_len, dim = q_in.shape
+                acc_ref, max_ref, sum_ref, stat_ref, dqt_ref, send_sem, recv_sem):
+    n_chip, n_half, n_grp, blk_len, dim = q_all.shape
     chunk = n_half * blk_len
     n_dev = 2 * n_chip
     rows2 = n_grp * blk_len
@@ -56,16 +61,19 @@
         pl.semaphore_signal(barrier, inc=1, device_id={'ctx': lax.rem(me + step, n_dev)}, device_id_type=MESH)
     pl.semaphore_wait(barrier, n_dev - 1)
 
+    def part(ref, g, t):
+        return ref.at[g, :, pl.ds(pl.multiple_of(t * blk_len, blk_len), blk_len), :]
+
     def send_kv(kind, s):
         src, dst = ((k_in, k_all), (v_in, v_all))[kind]
         return remote(kind, s, src.at[ahead(s)], dst.at[0, chip], ahead(s), core)
 
     def send_q(kind, s, t):
         src, dst = ((q_in, q_all), (do_in, do_all))[kind - Q]
-        return remote(kind, 2 * s + t, src.at[ahead(s), t], dst.at[chip, t], ahead(s), lax.rem(core + t, 2))
+        return remote(kind, 2 * s + t, part(src, ahead(s), t), dst.at[chip, t], ahead(s), lax.rem(core + t, 2))
 
     own_copies = (local(K, 0, k_in.at[chip], k_all.at[0, chip]), local(V, 0, v_in.at[chip], v_all.at[0, chip]),
-                  local(Q, 0, q_in.at[chip, 0], q_all.at[chip, 0]), local(DO, 0, do_in.at[chip, 0], do_all.at[chip, 0]))
+                  local(Q, 0, part(q_in, chip, 0), q_all.at[chip, 0]), local(DO, 0, part(do_in, chip, 0), do_all.at[chip, 0]))
     sends = []
     for s in (1, 3, 2):
         sends += [send_kv(K, s), send_kv(V, s)]
@@ -122,8 +130,6 @@
         rows = pl.ds(pl.multiple_of(lax.rem(kb, n_half) * blk_len, blk_len), blk_len)
         return lax.rem(chk + core, 2), chk // 2, rows
 
-    tok_q = lax.rem(lax.broadcasted_iota(jnp.int32, (rows2, blk_len), 0), blk_len)
-    tok_k = lax.broadcasted_iota(jnp.int32, (rows2, blk_len), 1)
     tok_qt = lax.rem(lax.broadcasted_iota(jnp.int32, (blk_len, rows2), 1), blk_len)
     tok_kt = lax.broadcasted_iota(jnp.int32, (blk_len, rows2), 0)
 
@@ -140,42 +146,54 @@
 
         @pl.when(jnp.logical_not(is_own))
         def _():
-            remote(Q, idx, q_in.at[0, 0], q_all.at[m, u], chip, core).wait_recv()
+            remote(Q, idx, part(q_in, 0, 0), q_all.at[m, u], chip, core).wait_recv()
 
         blk = block_of(s, u)
 
         def fwd(kb, kind):
             side, mk, krows = kv_slot(kb)
-            sc = dot_nt(q_all[m, u].reshape(rows2, dim), k_all[side, mk, krows, :])
-            if kind == 'diag':
-                sc = jnp.where(tok_k <= tok_q, sc, NEG_BIG)
-            elif kind == 'far':
-                sc = jnp.where(tok_k > tok_q, sc, NEG_BIG)
-            s_max = jnp.max(sc, axis=1, keepdims=True)
-            if kind == 'diag':
-                m_new = jnp.broadcast_to(s_max, (rows2, 128))
-            else:
-                m_old = m_ref[...]
-                m_new = jnp.maximum(m_old, s_max)
-                alpha = jnp.exp2((m_old - m_new) * coef)
-            p = jnp.exp2(sc * coef - (m_new * coef)[:, :1])
-            p_sum = jnp.sum(p, axis=1, keepdims=True)
-            pv = dot_nn(p.astype(jnp.bfloat16), v_all[side, mk, krows, :])
-            m_ref[...] = m_new
-            if kind == 'diag':
-                l_ref[...] = jnp.broadcast_to(p_sum, (rows2, 128))
-                acc_ref[...] = pv
-            else:
-                l_ref[...] = l_ref[...] * alpha + p_sum
-                acc_ref[...] = acc_ref[...] * alpha[:, :1] + pv
+            q2 = q_all[m, u].reshape(rows2, dim)
+            k_blk, v_blk = k_all[side, mk, krows, :], v_all[side, mk, krows, :]
+            cols = [slice(c * COLS, (c + 1) * COLS) for c in range(rows2 // COLS)]
+
+            def scores(c):
+                st = dot_nt(k_blk, q2[c])
+                if kind == 'diag':
+                    st = jnp.where(tok_kt[:, c] <= tok_qt[:, c], st, NEG_BIG)
+                elif kind == 'far':
+                    st = jnp.where(tok_kt[:, c] > tok_qt[:, c], st, NEG_BIG)
+                return st
+
+            def weigh(c, st):
+                m_new = jnp.max(st, axis=0, keepdims=True)
+                if kind != 'diag':
+                    m_old = max_ref[:, c]
+                    m_new = jnp.maximum(m_old, m_new)
+                    alpha = jnp.exp2((m_old - m_new) * coef)
+                p = jnp.exp2(st * coef - m_new * coef)
+                p_sum = jnp.sum(p, axis=0, keepdims=True)
+                pv = dot_tn(v_blk, p.astype(jnp.bfloat16))
+                max_ref[:, c] = m_new
+                if kind == 'diag':
+                    sum_ref[:, c] = p_sum
+                    acc_ref[:, c] = pv
+                else:
+                    sum_ref[:, c] = sum_ref[:, c] * alpha + p_sum
+                    acc_ref[:, c] = acc_ref[:, c] * alpha + pv
+
+            ready = scores(cols[0])
+            for here, after in zip(cols, cols[1:] + [None]):
+                then = scores(after) if after is not None else None
+                weigh(here, ready)
+                ready = then
 
         fwd(blk, 'diag')
         lax.fori_loop(jnp.maximum(blk - win + 1, 0), blk, lambda kb, c: (fwd(kb, 'full'), c)[1], 0)
         pl.when(blk >= win)(lambda: fwd(blk - win, 'far'))
 
-        l_tot = l_ref[...]
-        o_all[m, u] = (acc_ref[...] * (1.0 / l_tot)[:, :1]).astype(jnp.bfloat16).reshape(n_grp, blk_len, dim)
-        stat_ref[idx, 0:1, :] = jnp.transpose(m_ref[...] * coef + jnp.log2(l_tot))[0:1, :]
+        total = sum_ref[...]
+        o_all[m, u] = jnp.transpose(acc_ref[...] * (1.0 / total)).astype(jnp.bfloat16).reshape(n_grp, blk_len, dim)
+        stat_ref[idx, 0:1, :] = max_ref[...] * coef + jnp.log2(total)
         send_back(O, s, u)
 
     def send_back(kind, s, u):
@@ -184,11 +202,11 @@
 
         @pl.when(idx == 0)
         def _():
-            local(kind, 0, buf.at[chip, 0], out.at[chip, 0]).start()
+            local(kind, 0, buf.at[chip, 0], part(out, chip, 0)).start()
 
         @pl.when(idx > 0)
         def _():
-            remote(kind, idx, buf.at[m, u], out.at[chip, u], m, lax.rem(core + u, 2)).start()
+            remote(kind, idx, buf.at[m, u], part(out, chip, u), m, lax.rem(core + u, 2)).start()
 
     def bwd_unit(s, u, kv_chip, first, last):
         m, idx = behind(s), 2 * s + u
@@ -202,7 +220,7 @@
 
             @pl.when(idx > 0)
             def _():
-                remote(DO, idx, do_in.at[0, 0], do_all.at[m, u], chip, core).wait_recv()
+                remote(DO, idx, part(do_in, 0, 0), do_all.at[m, u], chip, core).wait_recv()
             both = do_all[m, u].reshape(rows2, dim).astype(jnp.float32) * o_all[m, u].reshape(rows2, dim).astype(jnp.float32)
             drow = jnp.sum(both, axis=1, keepdims=True)
             stat_ref[idx, 1:2, :] = jnp.transpose(jnp.broadcast_to(drow, (rows2, 128)))[0:1, :]
@@ -246,13 +264,13 @@
 
     def settle(s):
         m = behind(s)
-        for kind, part, other, buf, out, mul in ((DK, dk_all, dkx, k_all, dk_out, scale), (DV, dv_all, dvx, v_all, dv_out, 1.0)):
+        for kind, mine, other, buf, out, mul in ((DK, dk_all, dkx, k_all, dk_out, scale), (DV, dv_all, dvx, v_all, dv_out, 1.0)):
             swap(kind + 2, s).wait_recv()
             pass_on(kind - DK + KX, s).wait_send()
 
             def add_body(r, carry):
                 rows = pl.ds(pl.multiple_of(r * 256, 256), 256)
-                buf[0, m, rows, :] = ((part[0, m, rows, :] + other[m, rows, :]) * mul).astype(jnp.bfloat16)
+                buf[0, m, rows, :] = ((mine[0, m, rows, :] + other[m, rows, :]) * mul).astype(jnp.bfloat16)
                 return carry
             lax.fori_loop(0, chunk // 256, add_body, 0)
 
@@ -314,10 +332,10 @@
         for kind, buf, out in ((O, o_all, o_out), (DQ, dq_all, dq_out)):
             for t in range(2):
                 if s == 0 and t == 0:
-                    local(kind, 0, buf.at[chip, 0], out.at[chip, 0]).wait()
+                    local(kind, 0, buf.at[chip, 0], part(out, chip, 0)).wait()
                 else:
-                    remote(kind, 2 * s + t, buf.at[m, t], out.at[chip, t], m, lax.rem(core + t, 2)).wait_send()
-                    remote(kind, 2 * s + t, buf.at[m, t], out.at[h, t], m, core).wait_recv()
+                    remote(kind, 2 * s + t, buf.at[m, t], part(out, chip, t), m, lax.rem(core + t, 2)).wait_send()
+                    remote(kind, 2 * s + t, buf.at[m, t], part(out, h, t), m, core).wait_recv()
         for kind, buf, out in ((DK, k_all, dk_out), (DV, v_all, dv_out)):
             if s == 0:
                 local(kind, 0, buf.at[0, chip], out.at[chip]).wait()
@@ -339,13 +357,13 @@
         bf16, f32 = jnp.bfloat16, jnp.float32
 
         def split_q(x):
-            return jnp.transpose(x.reshape(2, blk_len, kv_heads, n_grp, dim), (2, 0, 3, 1, 4))
+            return jnp.transpose(x.reshape(chunk, kv_heads, n_grp, dim), (1, 2, 0, 3))
 
         def split_kv(x):
             return jnp.transpose(x.reshape(chunk, kv_heads, dim), (1, 0, 2))
 
         q_shape, kv_shape = (n_chip, 2, n_grp, blk_len, dim), (n_chip, chunk, dim)
-        q_type, kv_type = jax.ShapeDtypeStruct(q_shape, bf16), jax.ShapeDtypeStruct(kv_shape, bf16)
+        q_type, kv_type = jax.ShapeDtypeStruct((n_chip, n_grp, chunk, dim), bf16), jax.ShapeDtypeStruct(kv_shape, bf16)
         o_all, dq_all, dk_all, dv_all = pl.pallas_call(
             attn_kernel,
             out_shape=(q_type, q_type, kv_type, kv_type),
@@ -363,9 +381,9 @@
                 pltpu.VMEM(q_shape, bf16),
                 pltpu.VMEM(kv_shape, f32),
                 pltpu.VMEM(kv_shape, f32),
-                pltpu.VMEM((rows, dim), f32),
-                pltpu.VMEM((rows, 128), f32),
-                pltpu.VMEM((rows, 128), f32),
+                pltpu.VMEM((dim, rows), f32),
+                pltpu.VMEM((1, rows), f32),
+                pltpu.VMEM((1, rows), f32),
                 pltpu.VMEM((2 * n_chip, 8, rows), f32),
                 pltpu.VMEM((2, dim, rows), f32),
                 pltpu.SemaphoreType.DMA((12, 8)),
@@ -375,7 +393,7 @@
         )(split_q(q_loc), split_q(do_loc), split_kv(k_loc), split_kv(v_loc))
 
         def join_q(x):
-            return jnp.transpose(x, (1, 3, 0, 2, 4)).reshape(q_loc.shape)
+            return jnp.transpose(x, (2, 0, 1, 3)).reshape(q_loc.shape)
 
         def join_kv(x):
             return jnp.transpose(x, (1, 0, 2)).reshape(k_loc.shape)

time: 354 us -> 307 us (0.87)
  Pallas kernels: 325 us -> 278 us
    pallas_call x1, Pallas kernels: 325 us -> 278 us  [local_attn(): pl.pallas_call(attn_kernel, out_shape=(q_type, q_type, kv_type, kv_type),...]
    transpose x3 -> x0, local copies, waits for them, and re-layouts: 6.87 us -> none  [the longest x1 4.03 us: split_q(): jnp.transpose(x.reshape(2, blk_len, kv_heads, n_grp, dim), (2, 0, 3, 1, 4))]
    unnamed x18, local copies, waits for them, and re-layouts: 19.1 us -> 25.5 us
where the time goes in v4:
time: 307 us
  Pallas kernels  278 us (91%)
  local copies, waits for them, and re-layouts  28.1 us (9%)
    pallas_call x1, Pallas kernels, local_attn(): pl.pallas_call(attn_kernel, out_shape=(q_type, q_type, kv_type, kv_type),...  278 us
    unnamed x18, local copies, waits for them, and re-layouts  25.5 us

profile of v4, /device:TPU:113, one launch (start us, length us, event | category | flops | bytes accessed | tf_op | source)
XLA Modules:
  0.0 306.7 jit_solution(1701462058428548690)
XLA Ops:
  0.6 0.0 copy-start
  0.6 5.2 %copy.8 = bf16[1,1024,8,256]{3,1,2,0:T(8,128)(2,1)} copy(bf16[1,1024,8,256]{3,2,1,0:T(8,128)(2,1)} %param.4) | data formatting | bytes 8388608 | tf_op args[0]
  5.9 0.0 copy-done
  5.9 0.0 copy-start.4
  5.9 0.0 copy-start.5
  5.9 2.9 copy.9
  8.7 0.0 copy-done.4
  8.7 0.4 copy-done.5
  9.1 2.6 copy_bitcast_fusion
  11.7 277.9 %shard_map.75 = (bf16[4,2,1024,256]{3,2,1,0:T(8,128)(2,1)}, bf16[4,2,1024,256]{3,2,1,0:T(8,128)(2,1)}, bf16[4,1024,256]{2,1,0:T(8,128)(2,1)}, bf16[4,1024,256]{2,1,0:T(8,128)(2,1)}) custom-call(bf16[4,2,1024,256]{3,2,1,0:T(8,128)(2,1)} %bitcast.26, bf16[4,2,1024,256]{3,2,1,0:T(8,128)(2,1)} %bitcast.27, bf16[4,1024,256]{2,1,0:T(8,128)(2,1)} %get-tuple-element.17.k_in, ...), custom_call_target="tpu_custom_call" | custom-call | tf_op jit(solution)/shard_map/pallas_call | solution.py:367
  289.6 0.0 copy-start.1
  289.6 6.7 %copy.12 = bf16[1,1024,8,256]{3,2,1,0:T(8,128)(2,1)} copy(bf16[1,1024,8,256]{3,1,2,0:T(8,128)(2,1)} %bitcast.29) | data formatting | bytes 8388608
  296.3 0.0 copy-done.1
  296.3 0.0 copy-start.3
  296.3 4.4 %copy.13 = bf16[1,1024,8,256]{3,2,1,0:T(8,128)(2,1)} copy(bf16[1,1024,8,256]{3,1,2,0:T(8,128)(2,1)S(1)} %bitcast.28) | data formatting | bytes 8388608
  300.8 0.0 copy-done.3
  300.8 0.0 copy-start.2
  300.8 2.9 copy.14
  303.7 0.0 copy-done.2
  303.7 2.9 copy.15
Async XLA Ops:
  0.6 5.2 %copy-start = (bf16[1,1024,8,256]{3,2,1,0:T(8,128)(2,1)S(1)}, bf16[1,1024,8,256]{3,2,1,0:T(8,128)(2,1)}, u32[]{:S(2)}) copy-start(bf16[1,1024,8,256]{3,2,1,0:T(8,128)(2,1)} %param.7) | copy-start | bytes 12582916
  5.9 2.9 copy-start.4
  5.9 3.2 %copy-start.5 = (bf16[1,1024,4,256]{3,2,1,0:T(4,128)(2,1)S(1)}, bf16[1,1024,4,256]{3,2,1,0:T(4,128)(2,1)}, u32[]{:S(2)}) copy-start(bf16[1,1024,4,256]{3,2,1,0:T(4,128)(2,1)} %param.5) | copy-start | bytes 6291460
  289.6 6.7 %copy-start.1 = (bf16[4,2,1024,256]{3,2,1,0:T(8,128)(2,1)S(1)}, bf16[4,2,1024,256]{3,2,1,0:T(8,128)(2,1)}, u32[]{:S(2)}) copy-start(bf16[4,2,1024,256]{3,2,1,0:T(8,128)(2,1)} %get-tuple-element.9) | copy-start | bytes 12582916
  296.3 4.4 %copy-start.3 = (bf16[4,1024,256]{2,1,0:T(8,128)(2,1)S(1)}, bf16[4,1024,256]{2,1,0:T(8,128)(2,1)}, u32[]{:S(2)}) copy-start(bf16[4,1024,256]{2,1,0:T(8,128)(2,1)} %get-tuple-element.10) | copy-start | bytes 6291460
  300.8 2.9 copy-start.2

commit v5 on v4

--- a/solution.py
+++ b/solution.py
@@ -9,7 +9,7 @@
 
 WINDOW = 4096
 NEG_BIG = -1e30
-COLS = 256
+COLS = 512
 MESH = pl.DeviceIdType.MESH
 K, V, KX, VX, Q, DO, O, DQ, DK, DV, DKX, DVX = range(12)
 
@@ -28,7 +28,7 @@
 
 def attn_kernel(q_in, do_in, k_in, v_in, o_out, dq_out, dk_out, dv_out,
                 q_all, do_all, k_all, v_all, kt_all, dk_all, dv_all, o_all, dq_all, dkx, dvx,
-                acc_ref, max_ref, sum_ref, stat_ref, dqt_ref, send_sem, recv_sem):
+                acc_ref, s_ref, max_ref, sum_ref, stat_ref, dqt_ref, send_sem, recv_sem):
     n_chip, n_half, n_grp, blk_len, dim = q_all.shape
     chunk = n_half * blk_len
     n_dev = 2 * n_chip
@@ -150,21 +150,24 @@
 
         blk = block_of(s, u)
 
-        def fwd(kb, kind):
+        def fwd(kb, kind, kb_next):
             side, mk, krows = kv_slot(kb)
             q2 = q_all[m, u].reshape(rows2, dim)
-            k_blk, v_blk = k_all[side, mk, krows, :], v_all[side, mk, krows, :]
+            v_blk = v_all[side, mk, krows, :]
             cols = [slice(c * COLS, (c + 1) * COLS) for c in range(rows2 // COLS)]
 
-            def scores(c):
-                st = dot_nt(k_blk, q2[c])
+            def scores(kb_s, c):
+                side_s, mk_s, krows_s = kv_slot(kb_s)
+                return dot_nt(k_all[side_s, mk_s, krows_s, :], q2[c])
+
+            for c in cols:
+                st = scores(kb, c) if kind == 'diag' else s_ref[:, c]
                 if kind == 'diag':
                     st = jnp.where(tok_kt[:, c] <= tok_qt[:, c], st, NEG_BIG)
                 elif kind == 'far':
                     st = jnp.where(tok_kt[:, c] > tok_qt[:, c], st, NEG_BIG)
-                return st
-
-            def weigh(c, st):
+                if kb_next is not None:
+                    s_ref[:, c] = scores(kb_next, c)
                 m_new = jnp.max(st, axis=0, keepdims=True)
                 if kind != 'diag':
                     m_old = max_ref[:, c]
@@ -181,15 +184,11 @@
                     sum_ref[:, c] = sum_ref[:, c] * alpha + p_sum
                     acc_ref[:, c] = acc_ref[:, c] * alpha + pv
 
-            ready = scores(cols[0])
-            for here, after in zip(cols, cols[1:] + [None]):
-                then = scores(after) if after is not None else None
-                weigh(here, ready)
-                ready = then
-
-        fwd(blk, 'diag')
-        lax.fori_loop(jnp.maximum(blk - win + 1, 0), blk, lambda kb, c: (fwd(kb, 'full'), c)[1], 0)
-        pl.when(blk >= win)(lambda: fwd(blk - win, 'far'))
+        lo = jnp.maximum(blk - win + 1, 0)
+        far = jnp.maximum(blk - win, 0)
+        fwd(blk, 'diag', jnp.where(lo < blk, lo, far))
+        lax.fori_loop(lo, blk, lambda kb, c: (fwd(kb, 'full', jnp.where(kb + 1 < blk, kb + 1, far)), c)[1], 0)
+        pl.when(blk >= win)(lambda: fwd(blk - win, 'far', None))
 
         total = sum_ref[...]
         o_all[m, u] = jnp.transpose(acc_ref[...] * (1.0 / total)).astype(jnp.bfloat16).reshape(n_grp, blk_len, dim)
@@ -382,6 +381,7 @@
                 pltpu.VMEM(kv_shape, f32),
                 pltpu.VMEM(kv_shape, f32),
                 pltpu.VMEM((dim, rows), f32),
+                pltpu.VMEM((blk_len, rows), f32),
                 pltpu.VMEM((1, rows), f32),
                 pltpu.VMEM((1, rows), f32),
                 pltpu.VMEM((2 * n_chip, 8, rows), f32),

time: 307 us -> 307 us (level)
  no operation moved by 1% of the time
where the time goes in v5:
time: 307 us
  Pallas kernels  278 us (91%)
  local copies, waits for them, and re-layouts  28.1 us (9%)
    pallas_call x1, Pallas kernels, local_attn(): pl.pallas_call(attn_kernel, out_shape=(q_type, q_type, kv_type, kv_type),...  278 us
    unnamed x18, local copies, waits for them, and re-layouts  25.5 us

profile of v5, /device:TPU:113, one launch (start us, length us, event | category | flops | bytes accessed | tf_op | source)
XLA Modules:
  0.0 306.7 jit_solution(1586333178719441511)
XLA Ops:
  0.6 0.0 copy-start
  0.6 5.2 %copy.8 = bf16[1,1024,8,256]{3,1,2,0:T(8,128)(2,1)} copy(bf16[1,1024,8,256]{3,2,1,0:T(8,128)(2,1)} %param.4) | data formatting | bytes 8388608 | tf_op args[0]
  5.9 0.0 copy-done
  5.9 0.0 copy-start.4
  5.9 0.0 copy-start.5
  5.9 2.9 copy.9
  8.7 0.0 copy-done.4
  8.7 0.4 copy-done.5
  9.1 2.6 copy_bitcast_fusion
  11.7 278.0 %shard_map.75 = (bf16[4,2,1024,256]{3,2,1,0:T(8,128)(2,1)}, bf16[4,2,1024,256]{3,2,1,0:T(8,128)(2,1)}, bf16[4,1024,256]{2,1,0:T(8,128)(2,1)}, bf16[4,1024,256]{2,1,0:T(8,128)(2,1)}) custom-call(bf16[4,2,1024,256]{3,2,1,0:T(8,128)(2,1)} %bitcast.26, bf16[4,2,1024,256]{3,2,1,0:T(8,128)(2,1)} %bitcast.27, bf16[4,1024,256]{2,1,0:T(8,128)(2,1)} %get-tuple-element.17.k_in, ...), custom_call_target="tpu_custom_call" | custom-call | tf_op jit(solution)/shard_map/pallas_call | solution.py:366
  289.6 0.0 copy-start.1
  289.6 6.7 %copy.12 = bf16[1,1024,8,256]{3,2,1,0:T(8,128)(2,1)} copy(bf16[1,1024,8,256]{3,1,2,0:T(8,128)(2,1)} %bitcast.29) | data formatting | bytes 8388608
  296.4 0.0 copy-done.1
  296.4 0.0 copy-start.3
  296.4 4.4 %copy.13 = bf16[1,1024,8,256]{3,2,1,0:T(8,128)(2,1)} copy(bf16[1,1024,8,256]{3,1,2,0:T(8,128)(2,1)S(1)} %bitcast.28) | data formatting | bytes 8388608
  300.8 0.0 copy-done.3
  300.8 0.0 copy-start.2
  300.8 2.9 copy.14
  303.7 0.0 copy-done.2
  303.7 2.9 copy.15
Async XLA Ops:
  0.6 5.2 %copy-start = (bf16[1,1024,8,256]{3,2,1,0:T(8,128)(2,1)S(1)}, bf16[1,1024,8,256]{3,2,1,0:T(8,128)(2,1)}, u32[]{:S(2)}) copy-start(bf16[1,1024,8,256]{3,2,1,0:T(8,128)(2,1)} %param.7) | copy-start | bytes 12582916
  5.9 2.9 copy-start.4
  5.9 3.2 %copy-start.5 = (bf16[1,1024,4,256]{3,2,1,0:T(4,128)(2,1)S(1)}, bf16[1,1024,4,256]{3,2,1,0:T(4,128)(2,1)}, u32[]{:S(2)}) copy-start(bf16[1,1024,4,256]{3,2,1,0:T(4,128)(2,1)} %param.5) | copy-start | bytes 6291460
  289.6 6.7 %copy-start.1 = (bf16[4,2,1024,256]{3,2,1,0:T(8,128)(2,1)S(1)}, bf16[4,2,1024,256]{3,2,1,0:T(8,128)(2,1)}, u32[]{:S(2)}) copy-start(bf16[4,2,1024,256]{3,2,1,0:T(8,128)(2,1)} %get-tuple-element.9) | copy-start | bytes 12582916
  296.4 4.4 %copy-start.3 = (bf16[4,1024,256]{2,1,0:T(8,128)(2,1)S(1)}, bf16[4,1024,256]{2,1,0:T(8,128)(2,1)}, u32[]{:S(2)}) copy-start(bf16[4,1024,256]{2,1,0:T(8,128)(2,1)} %get-tuple-element.10) | copy-start | bytes 6291460
  300.8 2.9 copy-start.2
